TPU v7x, 128 devices: a whole 4x4x4 slice. The times are simulated.
128 devices in a mesh: grid: 32 (over x_hi, z, y), band: 4 (over x_lo, core).
Axes of the slice: x: 4 (x_hi: 2, x_lo: 2; x = x_hi * 2 + x_lo), y: 4, z: 4, core: 2. Of those that a mesh axis runs over, the one named last changes fastest.
Arguments:
- orbitals: float32 [128, 16, 16, 512], P('grid', None, None, 'band'), may hold values from -80 to 80
- projectors: float32 [128, 16, 16, 512], P('grid', None, None, 'band'), may hold values from -0.046875 to 0.046875
- potential: float32 [128, 16, 16], P('grid'), may hold values from 0.3 to 3
Outputs:
- updated_orbitals: float32 [128, 16, 16, 512], P('grid', None, None, 'band')
- rayleigh_quotients: float32 [3, 512], P(None, 'band')
- residual_norms: float32 [3, 512], P(None, 'band')
All inputs are finite; a program needn't handle non-finite values.
Results may differ from a plain program's by a relative error of at most 0.00012.
Values sent between devices are 32-bit elements; how exact they have to be, the bound alone decides.
No kernel may reach another device: no remote copies, remote signals or barrier semaphores. Data moves between devices by JAX's collectives and lax.ppermute only.
A program may use at most 128 MiB of HBM per device.

v0:
```python
import jax
import jax.numpy as jnp
from jax import lax
from jax.sharding import Mesh
from jax.sharding import PartitionSpec as P

ITERS = 3
BAND = ("band_0", "band_1")


STENCIL = (-205.0 / 72.0, 8.0 / 5.0, -1.0 / 5.0, 8.0 / 315.0, -1.0 / 560.0)
STEP_LENGTH = 0.25
NORM_EPS = 1e-06
HIGHEST = lax.Precision.HIGHEST


def with_halo(block, sides, width):
    for axis, dim in sides:
        count = lax.axis_size(axis)
        forward = [(i, i + 1) for i in range(count - 1)]
        forward.append((count - 1, 0))
        backward = [(target, source) for source, target in forward]
        low = lax.ppermute(
            lax.slice_in_dim(block, block.shape[dim] - width, None, axis=dim), axis, forward
        )
        high = lax.ppermute(lax.slice_in_dim(block, 0, width, axis=dim), axis, backward)
        block = jnp.concatenate([low, block, high], axis=dim)
    return block


def from_everyone(x, axis):
    copies = jnp.broadcast_to(x, (lax.axis_size(axis), *x.shape))
    return lax.all_to_all(copies, axis, split_axis=0, concat_axis=0, tiled=True)


def joined_along(pieces, dim):
    dims = list(pieces.shape[1:])
    dims[dim] *= pieces.shape[0]
    return jnp.moveaxis(pieces, 0, dim).reshape(dims)


def gathered_by_axis(x, axes, dim):
    far, near = axes
    initial = from_everyone(x, far)
    pieces = jnp.swapaxes(from_everyone(initial, near), 0, 1)
    return joined_along(pieces.reshape(-1, *x.shape), dim)


def rows_for(lines, count):
    spare = -len(lines) % count
    return jnp.pad(lines, [(0, spare)] + [(0, 0)] * (lines.ndim - 1))


def collect(x, axis, dim):
    pieces = from_everyone(x, axis)
    return joined_along(pieces, dim)


def cut_along(x, dim, count):
    before, after = (x.shape[:dim], x.shape[dim + 1 :])
    return jnp.moveaxis(x.reshape(*before, count, -1, *after), dim, 0)


def sum_at_owner(x, axis, dim):
    pieces = cut_along(x, dim, lax.axis_size(axis))
    arrived = lax.all_to_all(pieces, axis, split_axis=0, concat_axis=0, tiled=True)
    return arrived.sum(axis=0)


def nested_sum(x, axes):
    lines = x.reshape(-1, x.shape[-1])
    padded = rows_for(lines, lax.axis_size(axes))
    whole = collect(sum_at_owner(padded, axes, 0), axes, 0)
    return lax.slice_in_dim(whole, 0, len(lines)).reshape(x.shape)


def over_copies(x, axis):
    return from_everyone(x, axis).sum(axis=0)


def together(arrays, axis):
    ends = [0]
    for a in arrays:
        ends.append(ends[-1] + a.size)
    subtotal = over_copies(jnp.concatenate([a.ravel() for a in arrays]), axis)
    return tuple((subtotal[b:e].reshape(a.shape) for a, b, e in zip(arrays, ends, ends[1:])))


def matmul(left, right):
    return jnp.dot(left, right, precision=HIGHEST, preferred_element_type=jnp.float32)


def laplacian(grid_field):
    padded = with_halo(grid_field, (("grid", 0),), 4)
    planes_here = grid_field.shape[0]
    result = 3.0 * STENCIL[0] * grid_field
    for distance in range(1, 5):
        result = result + STENCIL[distance] * (
            padded[4 + distance : 4 + distance + planes_here]
            + padded[4 - distance : 4 - distance + planes_here]
        )
    for dimension in (1, 2):
        for distance in range(1, 5):
            result = result + STENCIL[distance] * (
                jnp.roll(grid_field, distance, dimension)
                + jnp.roll(grid_field, -distance, dimension)
            )
    return result


def local(orbitals, projectors, potential):
    grid_shape = orbitals.shape
    local_bands = orbitals.shape[3]
    total_bands = local_bands * lax.axis_size(BAND)
    first_band = lax.axis_index(BAND) * local_bands
    vectors = orbitals.reshape(-1, local_bands)
    every_projector = gathered_by_axis(projectors, ("band_0", "band_1"), 3).reshape(
        -1, projectors.shape[3] * lax.axis_size(BAND)
    )
    identity_matrix = jnp.eye(total_bands, dtype=jnp.float32)
    quotient_list = []
    norm_list = []
    for iteration in range(ITERS):
        gathered = gathered_by_axis(vectors.reshape(grid_shape), ("band_0", "band_1"), 3).reshape(
            -1, total_bands
        )
        own_rows = nested_sum(matmul(vectors.T, gathered), "grid")
        margin = collect(own_rows, BAND, 0)
        factor = jnp.linalg.cholesky(margin)
        inverse = jax.scipy.linalg.solve_triangular(factor, identity_matrix, lower=True)
        transform = inverse.T
        vectors = matmul(gathered, lax.dynamic_slice_in_dim(transform, first_band, local_bands, 1))
        coupling = nested_sum(matmul(every_projector.T, vectors), "grid")
        exchange_part = matmul(every_projector, coupling)
        grid_field = vectors.reshape(grid_shape)
        applied = (-0.5 * laplacian(grid_field) + potential[..., None] * grid_field).reshape(
            -1, local_bands
        ) - exchange_part
        rayleigh, energy, weight = together(
            (
                jnp.sum(vectors * applied, axis=0),
                jnp.sum(applied * applied, axis=0),
                jnp.sum(vectors * vectors, axis=0),
            ),
            "grid",
        )
        residual = applied - rayleigh[None, :] * vectors
        squared = energy - 2.0 * rayleigh * rayleigh + rayleigh * rayleigh * weight
        vectors = vectors - STEP_LENGTH * residual / jnp.sqrt(squared + NORM_EPS)[None, :]
        quotient_list.append(rayleigh)
        norm_list.append(jnp.sqrt(squared))
    return (vectors.reshape(grid_shape), jnp.stack(quotient_list), jnp.stack(norm_list))


def solution(mesh):
    finer = Mesh(mesh.devices.reshape(mesh.shape["grid"], 2, 2), ("grid", "band_0", "band_1"))
    placed = (P("grid", None, None, BAND), P("grid", None, None, BAND), P("grid", None, None))
    return jax.shard_map(
        local,
        mesh=finer,
        in_specs=placed,
        out_specs=(P("grid", None, None, BAND), P(None, BAND), P(None, BAND)),
        check_vma=False,
    )
```

profile of v0, /device:TPU:0, one launch (start us, length us, event | category | flops | bytes accessed | tf_op | source)
XLA Modules:
  0.0 988.0 jit_solution(6073977351899208240)
XLA Ops:
  6.8 13.3 %all-to-all-done = f32[2,4,16,16,128]{4,3,2,1,0:T(8,128)S(1)} async-done(((f32[2,4,16,16,128]{4,3,2,1,0:T(8,128)}), f32[2,4,16,16,128]{4,3,2,1,0:T(8,128)S(1)}, u32[]{:S(2)}, u32[]{:S(2)}) %all-to-all-start) | async-done | bytes 1048608 | tf_op jit(solution)/shard_map/all_to_all | solution.py:33
  34.6 21.7 %all_to_all.134 = f32[32,4,512]{2,1,0:T(4,128)S(1)} all-to-all(f32[32,4,512]{2,1,0:T(4,128)S(1)} %copy.251), channel_id=1, replica_groups=mesh['grid'=32,'band_0'=2,'band_1'=2] {'grid'}, dimensions={0} | all-to-all | bytes 524288 | tf_op jit(solution)/shard_map/all_to_all | solution.py:66
  61.0 12.4 %all-to-all-done.5 = f32[2,4,16,16,128]{4,3,2,1,0:T(8,128)S(1)} async-done(((f32[2,4,16,16,128]{4,3,2,1,0:T(8,128)}), f32[2,4,16,16,128]{4,3,2,1,0:T(8,128)S(1)}, u32[]{:S(2)}, u32[]{:S(2)}) %all-to-all-start.5) | async-done | bytes 1048608 | tf_op jit(solution)/shard_map/all_to_all | solution.py:33
  73.4 14.7 %all_to_all.135 = f32[32,4,512]{2,1,0:T(4,128)S(1)} all-to-all(f32[32,4,512]{2,1,0:T(4,128)S(1)} %broadcast_in_dim.78), channel_id=1, replica_groups=mesh['grid'=32,'band_0'=2,'band_1'=2] {'grid'}, dimensions={0} | all-to-all | bytes 524288 | tf_op jit(solution)/shard_map/all_to_all | solution.py:33
  103.8 12.3 %all-to-all-done.4 = f32[4,128,512]{1,2,0:T(8,128)} async-done(((f32[4,128,512]{1,2,0:T(8,128)}), f32[4,128,512]{1,2,0:T(8,128)}, u32[]{:S(2)}, u32[]{:S(2)}) %all-to-all-start.4) | async-done | bytes 1048608 | tf_op jit(solution)/shard_map/all_to_all | solution.py:33
  123.7 11.7 %cholesky.374 = f32[128,128]{1,0:T(8,128)S(1)} custom-call(f32[128,128]{1,0:T(8,128)S(1)} %cholesky.586), custom_call_target="Cholesky" | custom-call | tf_op jit(solution)/shard_map/jit(cholesky)/cholesky | solution.py:129
  149.6 11.9 %cholesky.393 = f32[128,128]{1,0:T(8,128)S(1)} custom-call(f32[128,128]{1,0:T(8,128)S(1)} %cholesky.590), custom_call_target="Cholesky" | custom-call | tf_op jit(solution)/shard_map/jit(cholesky)/cholesky | solution.py:129
  174.3 11.7 %cholesky.414 = f32[128,128]{1,0:T(8,128)S(1)} custom-call(f32[128,128]{1,0:T(8,128)S(1)} %cholesky.595), custom_call_target="Cholesky" | custom-call | tf_op jit(solution)/shard_map/jit(cholesky)/cholesky | solution.py:129
  198.7 11.9 %cholesky.431 = f32[128,128]{1,0:T(8,128)S(1)} custom-call(f32[128,128]{1,0:T(8,128)S(1)} %convolution_subtract_fusion.17), custom_call_target="Cholesky" | custom-call | tf_op jit(solution)/shard_map/jit(cholesky)/cholesky | solution.py:129
  218.1 11.9 %while.6 = (s32[]{:T(128)}, f32[512,512]{1,0:T(8,128)}, s32[4,2]{0,1:T(2,128)S(1)}, f32[4,128,128]{2,1,0:T(8,128)S(1)}, s32[]{:T(128)}) while((s32[]{:T(128)}, f32[512,512]{1,0:T(8,128)}, s32[4,2]{0,1:T(2,128)S(1)}, f32[4,128,128]{2,1,0:T(8,128)S(1)}, s32[]{:T(128)}) %tuple.146), condition=%wide.while_cond, body=%wide.while_body.sunk | while | flops 2 | bytes 131181 | solution.py:130
  230.7 40.1 %custom-call.34 = f32[4,128,128]{1,2,0:T(8,128)S(1)} custom-call(f32[4,128,128]{2,1,0:T(8,128)} %copy-done.14), custom_call_target="InvertDiagBlocksLowerTriangular" | custom-call | tf_op jit(solution)/shard_map/jit(_solve_triangular)/triangular_solve | solution.py:130
  336.2 16.2 %all_to_all.140 = f32[32,1,384]{2,1,0:T(1,128)S(1)} all-to-all(f32[32,1,384]{2,1,0:T(1,128)S(1)} %broadcast_in_dim.83), channel_id=1, replica_groups=mesh['grid'=32,'band_0'=2,'band_1'=2] {'grid'}, dimensions={0} | all-to-all | bytes 98304 | tf_op jit(solution)/shard_map/all_to_all | solution.py:33
  388.1 14.3 %all_to_all.141 = f32[32,4,512]{2,1,0:T(4,128)S(1)} all-to-all(f32[32,4,512]{2,1,0:T(4,128)S(1)} %copy.266), channel_id=1, replica_groups=mesh['grid'=32,'band_0'=2,'band_1'=2] {'grid'}, dimensions={0} | all-to-all | bytes 524288 | tf_op jit(solution)/shard_map/all_to_all | solution.py:66
  402.4 14.2 %all_to_all.137 = f32[32,4,512]{2,1,0:T(4,128)S(1)} all-to-all(f32[32,4,512]{2,1,0:T(4,128)S(1)} %broadcast_in_dim.86), channel_id=1, replica_groups=mesh['grid'=32,'band_0'=2,'band_1'=2] {'grid'}, dimensions={0} | all-to-all | bytes 524288 | tf_op jit(solution)/shard_map/all_to_all | solution.py:33
  421.6 14.2 %all-to-all-done.14 = f32[4,128,512]{1,2,0:T(8,128)S(1)} async-done(((f32[4,128,512]{1,2,0:T(8,128)}), f32[4,128,512]{1,2,0:T(8,128)S(1)}, u32[]{:S(2)}, u32[]{:S(2)}) %all-to-all-start.14) | async-done | bytes 1048608 | tf_op jit(solution)/shard_map/all_to_all | solution.py:33
  441.9 11.7 %cholesky.446 = f32[128,128]{1,0:T(8,128)S(1)} custom-call(f32[128,128]{1,0:T(8,128)S(1)} %cholesky.599), custom_call_target="Cholesky" | custom-call | tf_op jit(solution)/shard_map/jit(cholesky)/cholesky | solution.py:129
  466.1 11.7 %cholesky.465 = f32[128,128]{1,0:T(8,128)S(1)} custom-call(f32[128,128]{1,0:T(8,128)S(1)} %cholesky.603), custom_call_target="Cholesky" | custom-call | tf_op jit(solution)/shard_map/jit(cholesky)/cholesky | solution.py:129
  491.7 11.7 %cholesky.486 = f32[128,128]{1,0:T(8,128)S(1)} custom-call(f32[128,128]{1,0:T(8,128)S(1)} %cholesky.608), custom_call_target="Cholesky" | custom-call | tf_op jit(solution)/shard_map/jit(cholesky)/cholesky | solution.py:129
  516.8 11.7 %cholesky.503 = f32[128,128]{1,0:T(8,128)S(1)} custom-call(f32[128,128]{1,0:T(8,128)S(1)} %convolution_subtract_fusion.16), custom_call_target="Cholesky" | custom-call | tf_op jit(solution)/shard_map/jit(cholesky)/cholesky | solution.py:129
  535.0 11.9 %while.7 = (s32[]{:T(128)}, f32[512,512]{1,0:T(8,128)}, s32[4,2]{0,1:T(2,128)S(1)}, f32[4,128,128]{2,1,0:T(8,128)S(1)}, s32[]{:T(128)}) while((s32[]{:T(128)}, f32[512,512]{1,0:T(8,128)}, s32[4,2]{0,1:T(2,128)S(1)}, f32[4,128,128]{2,1,0:T(8,128)S(1)}, s32[]{:T(128)}) %tuple.155), condition=%wide.while_cond.clone, body=%wide.while_body.clone.sunk | while | flops 2 | bytes 131181 | solution.py:130
  547.6 40.1 %custom-call.38 = f32[4,128,128]{1,2,0:T(8,128)S(1)} custom-call(f32[4,128,128]{2,1,0:T(8,128)} %copy-done.15), custom_call_target="InvertDiagBlocksLowerTriangular" | custom-call | tf_op jit(solution)/shard_map/jit(_solve_triangular)/triangular_solve | solution.py:130
  653.0 16.4 %all_to_all.142 = f32[32,1,384]{2,1,0:T(1,128)S(1)} all-to-all(f32[32,1,384]{2,1,0:T(1,128)S(1)} %broadcast_in_dim.89), channel_id=1, replica_groups=mesh['grid'=32,'band_0'=2,'band_1'=2] {'grid'}, dimensions={0} | all-to-all | bytes 98304 | tf_op jit(solution)/shard_map/all_to_all | solution.py:33
  705.0 14.3 %all_to_all.143 = f32[32,4,512]{2,1,0:T(4,128)S(1)} all-to-all(f32[32,4,512]{2,1,0:T(4,128)S(1)} %copy.281), channel_id=1, replica_groups=mesh['grid'=32,'band_0'=2,'band_1'=2] {'grid'}, dimensions={0} | all-to-all | bytes 524288 | tf_op jit(solution)/shard_map/all_to_all | solution.py:66
  719.3 14.2 %all_to_all.139 = f32[32,4,512]{2,1,0:T(4,128)S(1)} all-to-all(f32[32,4,512]{2,1,0:T(4,128)S(1)} %broadcast_in_dim.92), channel_id=1, replica_groups=mesh['grid'=32,'band_0'=2,'band_1'=2] {'grid'}, dimensions={0} | all-to-all | bytes 524288 | tf_op jit(solution)/shard_map/all_to_all | solution.py:33
  733.9 16.9 %all_to_all.144 = f32[4,128,512]{1,2,0:T(8,128)S(1)} all-to-all(f32[4,128,512]{1,2,0:T(8,128)S(1)} %broadcast_in_dim.93), channel_id=1, replica_groups=mesh['grid'=32,'band_0'=2,'band_1'=2] {'band_0','band_1'}, dimensions={0} | all-to-all | bytes 2097152 | tf_op jit(solution)/shard_map/all_to_all | solution.py:33
  756.8 11.7 %cholesky.518 = f32[128,128]{1,0:T(8,128)S(1)} custom-call(f32[128,128]{1,0:T(8,128)S(1)} %cholesky.612), custom_call_target="Cholesky" | custom-call | tf_op jit(solution)/shard_map/jit(cholesky)/cholesky | solution.py:129
  781.0 11.7 %cholesky.537 = f32[128,128]{1,0:T(8,128)S(1)} custom-call(f32[128,128]{1,0:T(8,128)S(1)} %cholesky.616), custom_call_target="Cholesky" | custom-call | tf_op jit(solution)/shard_map/jit(cholesky)/cholesky | solution.py:129
  806.8 11.7 %cholesky.558 = f32[128,128]{1,0:T(8,128)S(1)} custom-call(f32[128,128]{1,0:T(8,128)S(1)} %cholesky.621), custom_call_target="Cholesky" | custom-call | tf_op jit(solution)/shard_map/jit(cholesky)/cholesky | solution.py:129
  831.8 11.7 %cholesky.575 = f32[128,128]{1,0:T(8,128)S(1)} custom-call(f32[128,128]{1,0:T(8,128)S(1)} %convolution_subtract_fusion.15), custom_call_target="Cholesky" | custom-call | tf_op jit(solution)/shard_map/jit(cholesky)/cholesky | solution.py:129
  849.8 11.9 %while.8 = (s32[]{:T(128)}, f32[512,512]{1,0:T(8,128)}, s32[4,2]{0,1:T(2,128)S(1)}, f32[4,128,128]{2,1,0:T(8,128)S(1)}, s32[]{:T(128)}) while((s32[]{:T(128)}, f32[512,512]{1,0:T(8,128)}, s32[4,2]{0,1:T(2,128)S(1)}, f32[4,128,128]{2,1,0:T(8,128)S(1)}, s32[]{:T(128)}) %tuple.156), condition=%wide.while_cond.clone.1, body=%wide.while_body.clone.1.sunk | while | flops 2 | bytes 131181 | solution.py:130
  862.4 40.1 %custom-call.42 = f32[4,128,128]{1,2,0:T(8,128)S(1)} custom-call(f32[4,128,128]{2,1,0:T(8,128)} %copy-done.16), custom_call_target="InvertDiagBlocksLowerTriangular" | custom-call | tf_op jit(solution)/shard_map/jit(_solve_triangular)/triangular_solve | solution.py:130
  967.8 16.4 %all_to_all.145 = f32[32,1,384]{2,1,0:T(1,128)S(1)} all-to-all(f32[32,1,384]{2,1,0:T(1,128)S(1)} %broadcast_in_dim.95), channel_id=1, replica_groups=mesh['grid'=32,'band_0'=2,'band_1'=2] {'grid'}, dimensions={0} | all-to-all | bytes 98304 | tf_op jit(solution)/shard_map/all_to_all | solution.py:33
  (359 shorter events, 505.5 us)
Async XLA Ops:
  0.6 5.8 copy-start.12
  2.8 17.3 %all-to-all-start = ((f32[2,4,16,16,128]{4,3,2,1,0:T(8,128)}), f32[2,4,16,16,128]{4,3,2,1,0:T(8,128)S(1)}, u32[]{:S(2)}, u32[]{:S(2)}) async-start(f32[2,4,16,16,128]{4,3,2,1,0:T(8,128)} %broadcast_in_dim.76), calls=%async_computation | async-start | bytes 2097152 | tf_op jit(solution)/shard_map/all_to_all | solution.py:33
  29.3 5.1 copy-start
  31.2 25.0 %copy-start.13 = (f32[4,16,16,128]{3,2,1,0:T(8,128)S(1)}, f32[4,16,16,128]{3,2,1,0:T(8,128)}, u32[]{:S(2)}) copy-start(f32[4,16,16,128]{3,2,1,0:T(8,128)} %param.7) | copy-start | bytes 1572868
  57.4 16.0 %all-to-all-start.5 = ((f32[2,4,16,16,128]{4,3,2,1,0:T(8,128)}), f32[2,4,16,16,128]{4,3,2,1,0:T(8,128)S(1)}, u32[]{:S(2)}, u32[]{:S(2)}) async-start(f32[2,4,16,16,128]{4,3,2,1,0:T(8,128)} %broadcast_in_dim.80), calls=%async_computation.5 | async-start | bytes 2097152 | tf_op jit(solution)/shard_map/all_to_all | solution.py:33
  89.6 6.6 all-to-all-start.6
  97.3 18.8 %all-to-all-start.4 = ((f32[4,128,512]{1,2,0:T(8,128)}), f32[4,128,512]{1,2,0:T(8,128)}, u32[]{:S(2)}, u32[]{:S(2)}) async-start(f32[4,128,512]{1,2,0:T(8,128)} %broadcast_in_dim.79), calls=%async_computation.4 | async-start | bytes 2097152 | tf_op jit(solution)/shard_map/all_to_all | solution.py:33
  102.2 172.7 %copy-start.4 = (f32[512,512]{1,0:T(8,128)}, f32[512,512]{1,0:T(8,128)S(1)}, u32[]{:S(2)}) copy-start(f32[512,512]{1,0:T(8,128)S(1)} %fusion.57) | copy-start | bytes 3145732
  122.7 1.0 copy-start.11
  272.5 4.4 copy-start.1
  285.6 36.8 %collective-permute-start = (f32[4,16,16,128]{3,2,1,0:T(8,128)S(1)}, f32[4,16,16,128]{3,2,1,0:T(8,128)}, u32[]{:S(2)}, u32[]{:S(2)}) collective-permute-start(f32[4,16,16,128]{3,2,1,0:T(8,128)S(1)} %bitcast.355), channel_id=1, source_target_pairs={{4,0},{8,4},{12,8},{16,12},{20,16},{24,20},{28,24},{32,28},{36,32}... | collective-permute-start | bytes 1572872 | tf_op jit(solution)/shard_map/ppermute | solution.py:26
  287.8 34.6 %collective-permute-start.1 = (f32[4,16,16,128]{3,2,1,0:T(8,128)S(1)}, f32[4,16,16,128]{3,2,1,0:T(8,128)}, u32[]{:S(2)}, u32[]{:S(2)}) collective-permute-start(f32[4,16,16,128]{3,2,1,0:T(8,128)S(1)} %bitcast.356), channel_id=1, source_target_pairs={{0,4},{4,8},{8,12},{12,16},{16,20},{20,24},{24,28},{28,32},{32,36}... | collective-permute-start | bytes 1572872 | tf_op jit(solution)/shard_map/ppermute | solution.py:23
  295.6 20.1 %all-to-all-start.7 = ((f32[32,16,128]{2,1,0:T(8,128)}), f32[32,16,128]{2,1,0:T(8,128)}, u32[]{:S(2)}, u32[]{:S(2)}) async-start(f32[32,16,128]{2,1,0:T(8,128)} %bitcast.23), calls=%async_computation.7 | async-start | bytes 524288 | tf_op jit(solution)/shard_map/all_to_all | solution.py:66
  317.4 15.1 %all-to-all-start.8 = ((f32[32,16,128]{2,1,0:T(8,128)}), f32[32,16,128]{2,1,0:T(8,128)}, u32[]{:S(2)}, u32[]{:S(2)}) async-start(f32[32,16,128]{2,1,0:T(8,128)} %broadcast_in_dim.82), calls=%async_computation.8 | async-start | bytes 524288 | tf_op jit(solution)/shard_map/all_to_all | solution.py:33
  355.6 14.4 %all-to-all-start.10 = ((f32[2,4,16,16,128]{4,3,2,1,0:T(8,128)}), f32[2,4,16,16,128]{4,3,2,1,0:T(8,128)}, u32[]{:S(2)}, u32[]{:S(2)}) async-start(f32[2,4,16,16,128]{4,3,2,1,0:T(8,128)} %broadcast_in_dim.84), calls=%async_computation.10 | async-start | bytes 2097152 | tf_op jit(solution)/shard_map/all_to_all | solution.py:33
  417.9 17.9 %all-to-all-start.14 = ((f32[4,128,512]{1,2,0:T(8,128)}), f32[4,128,512]{1,2,0:T(8,128)S(1)}, u32[]{:S(2)}, u32[]{:S(2)}) async-start(f32[4,128,512]{1,2,0:T(8,128)} %broadcast_in_dim.87), calls=%async_computation.14 | async-start | bytes 2097152 | tf_op jit(solution)/shard_map/all_to_all | solution.py:33
  491.7 96.1 %copy-start.5 = (f32[512,512]{1,0:T(8,128)S(1)}, f32[512,512]{1,0:T(8,128)}, u32[]{:S(2)}) copy-start(f32[512,512]{1,0:T(8,128)} %copy-done.4) | copy-start | bytes 3145732
  589.4 4.4 copy-start.2
  601.9 36.8 %collective-permute-start.2 = (f32[4,16,16,128]{3,2,1,0:T(8,128)S(1)}, f32[4,16,16,128]{3,2,1,0:T(8,128)}, u32[]{:S(2)}, u32[]{:S(2)}) collective-permute-start(f32[4,16,16,128]{3,2,1,0:T(8,128)S(1)} %bitcast.336), channel_id=1, source_target_pairs={{4,0},{8,4},{12,8},{16,12},{20,16},{24,20},{28,24},{32,28},{36,32}... | collective-permute-start | bytes 1572872 | tf_op jit(solution)/shard_map/ppermute | solution.py:26
  604.1 34.6 %collective-permute-start.3 = (f32[4,16,16,128]{3,2,1,0:T(8,128)S(1)}, f32[4,16,16,128]{3,2,1,0:T(8,128)}, u32[]{:S(2)}, u32[]{:S(2)}) collective-permute-start(f32[4,16,16,128]{3,2,1,0:T(8,128)S(1)} %bitcast.337), channel_id=1, source_target_pairs={{0,4},{4,8},{8,12},{12,16},{16,20},{20,24},{24,28},{28,32},{32,36}... | collective-permute-start | bytes 1572872 | tf_op jit(solution)/shard_map/ppermute | solution.py:23
  612.2 20.1 %all-to-all-start.15 = ((f32[32,16,128]{2,1,0:T(8,128)}), f32[32,16,128]{2,1,0:T(8,128)}, u32[]{:S(2)}, u32[]{:S(2)}) async-start(f32[32,16,128]{2,1,0:T(8,128)} %bitcast.45), calls=%async_computation.15 | async-start | bytes 524288 | tf_op jit(solution)/shard_map/all_to_all | solution.py:66
  634.0 15.3 %all-to-all-start.16 = ((f32[32,16,128]{2,1,0:T(8,128)}), f32[32,16,128]{2,1,0:T(8,128)}, u32[]{:S(2)}, u32[]{:S(2)}) async-start(f32[32,16,128]{2,1,0:T(8,128)} %broadcast_in_dim.88), calls=%async_computation.16 | async-start | bytes 524288 | tf_op jit(solution)/shard_map/all_to_all | solution.py:33
  672.5 14.4 %all-to-all-start.18 = ((f32[2,4,16,16,128]{4,3,2,1,0:T(8,128)}), f32[2,4,16,16,128]{4,3,2,1,0:T(8,128)}, u32[]{:S(2)}, u32[]{:S(2)}) async-start(f32[2,4,16,16,128]{4,3,2,1,0:T(8,128)} %broadcast_in_dim.90), calls=%async_computation.18 | async-start | bytes 2097152 | tf_op jit(solution)/shard_map/all_to_all | solution.py:33
  806.7 95.8 %copy-start.6 = (f32[512,512]{1,0:T(8,128)S(1)}, f32[512,512]{1,0:T(8,128)}, u32[]{:S(2)}) copy-start(f32[512,512]{1,0:T(8,128)} %copy-done.4) | copy-start | bytes 3145732
  904.2 4.4 copy-start.3
  916.7 36.9 %collective-permute-start.4 = (f32[4,16,16,128]{3,2,1,0:T(8,128)S(1)}, f32[4,16,16,128]{3,2,1,0:T(8,128)}, u32[]{:S(2)}, u32[]{:S(2)}) collective-permute-start(f32[4,16,16,128]{3,2,1,0:T(8,128)S(1)} %bitcast.317), channel_id=1, source_target_pairs={{4,0},{8,4},{12,8},{16,12},{20,16},{24,20},{28,24},{32,28},{36,32}... | collective-permute-start | bytes 1572872 | tf_op jit(solution)/shard_map/ppermute | solution.py:26
  918.8 34.8 %collective-permute-start.5 = (f32[4,16,16,128]{3,2,1,0:T(8,128)S(1)}, f32[4,16,16,128]{3,2,1,0:T(8,128)}, u32[]{:S(2)}, u32[]{:S(2)}) collective-permute-start(f32[4,16,16,128]{3,2,1,0:T(8,128)S(1)} %bitcast.318), channel_id=1, source_target_pairs={{0,4},{4,8},{8,12},{12,16},{16,20},{20,24},{24,28},{28,32},{32,36}... | collective-permute-start | bytes 1572872 | tf_op jit(solution)/shard_map/ppermute | solution.py:23
  926.9 20.1 %all-to-all-start.23 = ((f32[32,16,128]{2,1,0:T(8,128)}), f32[32,16,128]{2,1,0:T(8,128)}, u32[]{:S(2)}, u32[]{:S(2)}) async-start(f32[32,16,128]{2,1,0:T(8,128)} %bitcast.67), calls=%async_computation.23 | async-start | bytes 524288 | tf_op jit(solution)/shard_map/all_to_all | solution.py:66
  948.8 15.3 %all-to-all-start.24 = ((f32[32,16,128]{2,1,0:T(8,128)}), f32[32,16,128]{2,1,0:T(8,128)}, u32[]{:S(2)}, u32[]{:S(2)}) async-start(f32[32,16,128]{2,1,0:T(8,128)} %broadcast_in_dim.94), calls=%async_computation.24 | async-start | bytes 524288 | tf_op jit(solution)/shard_map/all_to_all | solution.py:33
  967.7 18.8 %copy-start.18 = (f32[1,128]{1,0:T(1,128)S(1)}, f32[1,128]{1,0:T(1,128)}, u32[]{:S(2)}) copy-start(f32[1,128]{1,0:T(1,128)} %get-tuple-element.202) | copy-start | bytes 1540
  967.8 18.8 %copy-start.19 = (f32[1,128]{1,0:T(1,128)S(1)}, f32[1,128]{1,0:T(1,128)}, u32[]{:S(2)}) copy-start(f32[1,128]{1,0:T(1,128)} %get-tuple-element.206) | copy-start | bytes 1540
  967.8 19.4 %copy-start.17 = (f32[1,128]{1,0:T(1,128)S(1)}, f32[1,128]{1,0:T(1,128)}, u32[]{:S(2)}) copy-start(f32[1,128]{1,0:T(1,128)} %get-tuple-element.200) | copy-start | bytes 1540
  (7 other events, 6.1 us)
where the time goes:
time: 998 us; the launch traced here: 988 us
  other arithmetic  402 us (40%)
  blocking collectives  175 us (18%)
  local copies, waits for them, and re-layouts  145 us (15%)
  waiting for transfers between devices  110 us (11%)
  starting transfers between devices  78 us (8%)
  matrix products  68.6 us (7%)
    another operation x44, other arithmetic, local(): factor = jnp.linalg.cholesky(margin)  242 us
    another operation x7, other arithmetic, local(): jax.scipy.linalg.solve_triangular(factor, identity_matrix, lower=True)  128 us
    all_to_all x10, blocking collectives, from_everyone(): return lax.all_to_all(copies, axis, split_axis=0, concat_axis=0, tiled=True)  125 us
    all_to_all x10, waiting for transfers between devices, from_everyone(): return lax.all_to_all(copies, axis, split_axis=0, concat_axis=0, tiled=True)  83.6 us
    all_to_all x3, blocking collectives, sum_at_owner(): lax.all_to_all(pieces, axis, split_axis=0, concat_axis=0, tiled=True)  50.2 us
    all_to_all x10, starting transfers between devices, from_everyone(): return lax.all_to_all(copies, axis, split_axis=0, concat_axis=0, tiled=True)  42.7 us
    slice x48, local copies, waits for them, and re-layouts, laplacian(): jnp.roll(grid_field, distance, dimension)  41.1 us
    another operation x40, local copies, waits for them, and re-layouts, local(): jax.scipy.linalg.solve_triangular(factor, identity_matrix, lower=True)  35.5 us
  transfers between devices with their start and end apart: 19, of which 13 were waited for; matrix products, arithmetic and copies ran while one was open for 6% of the time, Pallas kernels for 0%

commit v1 on v0

--- a/solution.py
+++ b/solution.py
@@ -1,6 +1,8 @@
 import jax
 import jax.numpy as jnp
 from jax import lax
+from jax.experimental import pallas as pl
+from jax.experimental.pallas import tpu as pltpu
 from jax.sharding import Mesh
 from jax.sharding import PartitionSpec as P
 
@@ -12,6 +14,86 @@
 STEP_LENGTH = 0.25
 NORM_EPS = 1e-06
 HIGHEST = lax.Precision.HIGHEST
+
+BLOCK = 128
+TILE = 8
+
+def dot_t(left, right):
+    return lax.dot_general(left, right, (((0,), (0,)), ((), ())), precision=HIGHEST,
+                           preferred_element_type=jnp.float32)
+
+def row_of(tile, j):
+    return jnp.broadcast_to(tile[j:j + 1, :], tile.shape)
+
+def lane_of(tile, j):
+    return jnp.broadcast_to(tile[:, j:j + 1], tile.shape)
+
+def inverse_factor(tiles):
+    count = len(tiles)
+    lane = lax.broadcasted_iota(jnp.int32, tiles[0].shape, 1)
+    sub = lax.broadcasted_iota(jnp.int32, tiles[0].shape, 0)
+    tiles = list(tiles)
+    for p in range(count):
+        base = TILE * p
+        inside = (lane >= base) & (lane < base + TILE)
+        head = [lane_of(tiles[p], base + j) for j in range(TILE)]
+        own = jnp.where(inside, (lane == base + sub).astype(jnp.float32), tiles[p])
+        rows, scales, crosses = [], [], []
+        for j in range(TILE):
+            scale = lax.rsqrt(row_of(head[j], j))
+            row = row_of(own, j) * scale
+            column = jnp.where(sub > j, head[j] * scale, 0.0)
+            own = jnp.where(sub == j, row, own - column * row)
+            cross = [None] * TILE
+            for k in range(j + 1, TILE):
+                cross[k] = row_of(head[k], j) * scale
+                head[k] = head[k] - column * cross[k]
+            rows.append(row)
+            scales.append(scale)
+            crosses.append(cross)
+        tiles[p] = jnp.where(lane < base + TILE, own, 0.0)
+        for t in range(p + 1, count):
+            parts = [lane_of(tiles[t], base + j) for j in range(TILE)]
+            tile = jnp.where(inside, 0.0, tiles[t])
+            for j in range(TILE):
+                column = parts[j] * scales[j]
+                tile = tile - column * rows[j]
+                for k in range(j + 1, TILE):
+                    parts[k] = parts[k] - column * crosses[j][k]
+            tiles[t] = tile
+    return tiles
+
+def factor_kernel(s_ref, x_ref):
+    size = s_ref.shape[0]
+    blocks = size // BLOCK
+    x_ref[...] = s_ref[...]
+    def step(k, carry):
+        here = pl.ds(pl.multiple_of(k * BLOCK, BLOCK), BLOCK)
+        tiles = [x_ref[pl.ds(pl.multiple_of(k * BLOCK + TILE * t, TILE), TILE), here] for t in range(BLOCK // TILE)]
+        own = jnp.concatenate(inverse_factor(tiles), axis=0)
+        x_ref[here, here] = jnp.eye(BLOCK, dtype=jnp.float32)
+        panel = jnp.dot(own, x_ref[here, :], precision=HIGHEST, preferred_element_type=jnp.float32)
+        x_ref[here, :] = panel
+        def update(i, carry):
+            there = pl.ds(pl.multiple_of(i * BLOCK, BLOCK), BLOCK)
+            x_ref[there, here] = jnp.zeros((BLOCK, BLOCK), jnp.float32)
+            x_ref[there, :] = x_ref[there, :] - dot_t(x_ref[here, there], x_ref[here, :])
+            return carry
+        return lax.fori_loop(k + 1, blocks, update, carry)
+    lax.fori_loop(0, blocks, step, 0)
+    row = lax.broadcasted_iota(jnp.int32, (size, size), 0)
+    column = lax.broadcasted_iota(jnp.int32, (size, size), 1)
+    x_ref[...] = jnp.where(row >= column, x_ref[...], 0.0)
+
+def inverse_cholesky(s):
+    return pl.pallas_call(
+        factor_kernel,
+        out_shape=jax.ShapeDtypeStruct(s.shape, jnp.float32),
+        in_specs=[pl.BlockSpec(memory_space=pltpu.VMEM)],
+        out_specs=pl.BlockSpec(memory_space=pltpu.VMEM),
+        name="inverse_factor",
+        cost_estimate=pl.CostEstimate(flops=20_000_000_000, bytes_accessed=2 * s.size * 4, transcendentals=s.shape[0]),
+    )(s)
 
 
 def with_halo(block, sides, width):
@@ -117,7 +199,6 @@
     every_projector = gathered_by_axis(projectors, ("band_0", "band_1"), 3).reshape(
         -1, projectors.shape[3] * lax.axis_size(BAND)
     )
-    identity_matrix = jnp.eye(total_bands, dtype=jnp.float32)
     quotient_list = []
     norm_list = []
     for iteration in range(ITERS):
@@ -126,8 +207,7 @@
         )
         own_rows = nested_sum(matmul(vectors.T, gathered), "grid")
         margin = collect(own_rows, BAND, 0)
-        factor = jnp.linalg.cholesky(margin)
-        inverse = jax.scipy.linalg.solve_triangular(factor, identity_matrix, lower=True)
+        inverse = inverse_cholesky(margin)
         transform = inverse.T
         vectors = matmul(gathered, lax.dynamic_slice_in_dim(transform, first_band, local_bands, 1))
         coupling = nested_sum(matmul(every_projector.T, vectors), "grid")

time: 998 us -> 594 us (0.60)
  other arithmetic: 402 us -> 26.6 us
  Pallas kernels: 0 us -> 67.3 us
  local copies, waits for them, and re-layouts: 145 us -> 88.3 us
  matrix products: 68.6 us -> 36.1 us
  blocking collectives: 175 us -> 195 us
  waiting for transfers between devices: 110 us -> 97.7 us
    another operation x52 -> x0, other arithmetic: 370 us -> none  [the longest x44 242 us: local(): factor = jnp.linalg.cholesky(margin)]
    pallas_call x0 -> x3, Pallas kernels: none -> 67.3 us  [inverse_cholesky(): pl.pallas_call(factor_kernel, out_shape=jax.ShapeDtypeStruct(s.shape, jnp...]
    another operation x39 -> x0, matrix products: 38.3 us -> none  [the longest x18 20.4 us: local(): factor = jnp.linalg.cholesky(margin)]
    another operation x52 -> x0, local copies, waits for them, and re-layouts: 36.9 us -> none  [the longest x40 35.5 us: local(): jax.scipy.linalg.solve_triangular(factor, identity_matrix, lower=True)]
    all_to_all x10 -> x11, blocking collectives: 125 us -> 144 us  [from_everyone(): return lax.all_to_all(copies, axis, split_axis=0, concat_axis=0, tiled=True)]
    reshape x12 -> x3, local copies, waits for them, and re-layouts: 12.9 us -> 0.27 us  [joined_along(): return jnp.moveaxis(pieces, 0, dim).reshape(dims)]
    all_to_all x10 -> x9, waiting for transfers between devices: 83.6 us -> 71.7 us  [from_everyone(): return lax.all_to_all(copies, axis, split_axis=0, concat_axis=0, tiled=True)]
    all_to_all x10 -> x9, starting transfers between devices: 42.7 us -> 38.1 us  [from_everyone(): return lax.all_to_all(copies, axis, split_axis=0, concat_axis=0, tiled=True)]
  transfers between devices with their start and end apart: 19 -> 18, of which waited for: 13 -> 12; matrix products, arithmetic and copies ran while one was open for 6% -> 9% of each run, Pallas kernels for 0% -> 0%
where the time goes in v1:
time: 594 us; the launch traced here: 586 us
  blocking collectives  195 us (33%)
  waiting for transfers between devices  97.7 us (16%)
  local copies, waits for them, and re-layouts  88.3 us (15%)
  starting transfers between devices  73.4 us (12%)
  Pallas kernels  67.3 us (11%)
  matrix products  36.1 us (6%)
  other arithmetic  26.6 us (4%)
    all_to_all x11, blocking collectives, from_everyone(): return lax.all_to_all(copies, axis, split_axis=0, concat_axis=0, tiled=True)  144 us
    all_to_all x9, waiting for transfers between devices, from_everyone(): return lax.all_to_all(copies, axis, split_axis=0, concat_axis=0, tiled=True)  71.7 us
    pallas_call x3, Pallas kernels, inverse_cholesky(): pl.pallas_call(factor_kernel, out_shape=jax.ShapeDtypeStruct(s.shape, jnp...  67.3 us
    all_to_all x3, blocking collectives, sum_at_owner(): lax.all_to_all(pieces, axis, split_axis=0, concat_axis=0, tiled=True)  50.4 us
    slice x48, local copies, waits for them, and re-layouts, laplacian(): jnp.roll(grid_field, distance, dimension)  40.9 us
    all_to_all x9, starting transfers between devices, from_everyone(): return lax.all_to_all(copies, axis, split_axis=0, concat_axis=0, tiled=True)  38.1 us
    dot_general x12, matrix products, matmul(): jnp.dot(left, right, precision=HIGHEST, preferred_element_type=jnp.float32)  36.1 us
    all_to_all x3, starting transfers between devices, sum_at_owner(): lax.all_to_all(pieces, axis, split_axis=0, concat_axis=0, tiled=True)  28.7 us
  transfers between devices with their start and end apart: 18, of which 12 were waited for; matrix products, arithmetic and copies ran while one was open for 9% of the time, Pallas kernels for 0%

profile of v1, /device:TPU:0, one launch (start us, length us, event | category | flops | bytes accessed | tf_op | source)
XLA Modules:
  0.0 585.9 jit_solution(288088675360292219)
XLA Ops:
  6.8 13.3 %all-to-all-done = f32[2,4,16,16,128]{4,3,2,1,0:T(8,128)S(1)} async-done(((f32[2,4,16,16,128]{4,3,2,1,0:T(8,128)}), f32[2,4,16,16,128]{4,3,2,1,0:T(8,128)S(1)}, u32[]{:S(2)}, u32[]{:S(2)}) %all-to-all-start) | async-done | bytes 1048608 | tf_op jit(solution)/shard_map/all_to_all | solution.py:115
  22.3 5.4 all_to_all.133
  34.7 21.7 %all_to_all.134 = f32[32,4,512]{2,1,0:T(4,128)S(1)} all-to-all(f32[32,4,512]{2,1,0:T(4,128)S(1)} %copy.215), channel_id=1, replica_groups=mesh['grid'=32,'band_0'=2,'band_1'=2] {'grid'}, dimensions={0} | all-to-all | bytes 524288 | tf_op jit(solution)/shard_map/all_to_all | solution.py:148
  61.1 12.4 %all-to-all-done.5 = f32[2,4,16,16,128]{4,3,2,1,0:T(8,128)S(1)} async-done(((f32[2,4,16,16,128]{4,3,2,1,0:T(8,128)}), f32[2,4,16,16,128]{4,3,2,1,0:T(8,128)S(1)}, u32[]{:S(2)}, u32[]{:S(2)}) %all-to-all-start.5) | async-done | bytes 1048608 | tf_op jit(solution)/shard_map/all_to_all | solution.py:115
  73.5 14.7 %all_to_all.135 = f32[32,4,512]{2,1,0:T(4,128)S(1)} all-to-all(f32[32,4,512]{2,1,0:T(4,128)S(1)} %broadcast_in_dim.77), channel_id=1, replica_groups=mesh['grid'=32,'band_0'=2,'band_1'=2] {'grid'}, dimensions={0} | all-to-all | bytes 524288 | tf_op jit(solution)/shard_map/all_to_all | solution.py:115
  102.8 12.8 %all-to-all-done.4 = f32[4,128,512]{2,1,0:T(8,128)S(1)} async-done(((f32[4,128,512]{2,1,0:T(8,128)}), f32[4,128,512]{2,1,0:T(8,128)S(1)}, u32[]{:S(2)}, u32[]{:S(2)}) %all-to-all-start.4) | async-done | bytes 1048608 | tf_op jit(solution)/shard_map/all_to_all | solution.py:115
  116.6 22.4 %inverse_factor.3 = f32[512,512]{1,0:T(8,128)} custom-call(f32[512,512]{1,0:T(8,128)} %bitcast.223), custom_call_target="tpu_custom_call" | custom-call | flops 20000000000 | bytes 2097152 | tf_op jit(solution)/shard_map/inverse_factor/pallas_call | solution.py:89
  159.3 9.6 %all-to-all-start.7 = ((f32[32,16,128]{2,1,0:T(8,128)}), f32[32,16,128]{2,1,0:T(8,128)}, u32[]{:S(2)}, u32[]{:S(2)}) async-start(f32[32,16,128]{2,1,0:T(8,128)} %bitcast.13), calls=%async_computation.7 | async-start | bytes 524288 | tf_op jit(solution)/shard_map/all_to_all | solution.py:148
  170.7 8.7 %all-to-all-done.7 = f32[32,16,128]{2,1,0:T(8,128)} async-done(((f32[32,16,128]{2,1,0:T(8,128)}), f32[32,16,128]{2,1,0:T(8,128)}, u32[]{:S(2)}, u32[]{:S(2)}) %all-to-all-start.7) | async-done | bytes 262176 | tf_op jit(solution)/shard_map/all_to_all | solution.py:148
  181.1 5.0 all-to-all-start.8
  186.1 6.2 %multiply_add_fusion.2 = f32[4,16,16,128]{3,2,1,0:T(8,128)} fusion(f32[4,16,16,128]{3,2,1,0:T(8,128)S(1)} %bitcast.199, f32[4,16,4,128]{3,2,1,0:T(4,128)} %get-tuple-element.112, f32[4,16,12,128]{3,2,1,0:T(8,128)} %get-tuple-element.114, f32[4,16,12,128]{3,2,1,0:T(8,128)} %get-tuple-element.113, f32[4,16,4,128]{3,2,1,0:T(4,128)} %get-tuple-element.111, ...), kind=kLoop, calls=%fused_computation.200 | loop fusion | flops 8126464 | bytes 10489856 | tf_op jit(solution)/shard_map/add | solution.py:216
  200.3 16.5 %all_to_all.136 = f32[32,1,384]{2,1,0:T(1,128)S(1)} all-to-all(f32[32,1,384]{2,1,0:T(1,128)S(1)} %broadcast_in_dim.82), channel_id=1, replica_groups=mesh['grid'=32,'band_0'=2,'band_1'=2] {'grid'}, dimensions={0} | all-to-all | bytes 98304 | tf_op jit(solution)/shard_map/all_to_all | solution.py:115
  223.9 11.3 %all-to-all-done.10 = f32[2,4,16,16,128]{4,3,2,1,0:T(8,128)} async-done(((f32[2,4,16,16,128]{4,3,2,1,0:T(8,128)}), f32[2,4,16,16,128]{4,3,2,1,0:T(8,128)}, u32[]{:S(2)}, u32[]{:S(2)}) %all-to-all-start.10) | async-done | bytes 1048608 | tf_op jit(solution)/shard_map/all_to_all | solution.py:115
  238.6 5.4 all_to_all.137
  253.3 14.4 %all_to_all.138 = f32[32,4,512]{2,1,0:T(4,128)S(1)} all-to-all(f32[32,4,512]{2,1,0:T(4,128)S(1)} %copy.227), channel_id=1, replica_groups=mesh['grid'=32,'band_0'=2,'band_1'=2] {'grid'}, dimensions={0} | all-to-all | bytes 524288 | tf_op jit(solution)/shard_map/all_to_all | solution.py:148
  267.9 14.2 %all_to_all.139 = f32[32,4,512]{2,1,0:T(4,128)S(1)} all-to-all(f32[32,4,512]{2,1,0:T(4,128)S(1)} %broadcast_in_dim.85), channel_id=1, replica_groups=mesh['grid'=32,'band_0'=2,'band_1'=2] {'grid'}, dimensions={0} | all-to-all | bytes 524288 | tf_op jit(solution)/shard_map/all_to_all | solution.py:115
  282.3 17.7 %all_to_all.140 = f32[4,128,512]{2,1,0:T(8,128)} all-to-all(f32[4,128,512]{2,1,0:T(8,128)S(1)} %broadcast_in_dim.86), channel_id=1, replica_groups=mesh['grid'=32,'band_0'=2,'band_1'=2] {'band_0','band_1'}, dimensions={0} | all-to-all | bytes 2097152 | tf_op jit(solution)/shard_map/all_to_all | solution.py:115
  300.1 22.4 %inverse_factor.4 = f32[512,512]{1,0:T(8,128)} custom-call(f32[512,512]{1,0:T(8,128)} %bitcast.224), custom_call_target="tpu_custom_call" | custom-call | flops 20000000000 | bytes 2097152 | tf_op jit(solution)/shard_map/inverse_factor/pallas_call | solution.py:89
  342.8 9.6 %all-to-all-start.15 = ((f32[32,16,128]{2,1,0:T(8,128)}), f32[32,16,128]{2,1,0:T(8,128)}, u32[]{:S(2)}, u32[]{:S(2)}) async-start(f32[32,16,128]{2,1,0:T(8,128)} %bitcast.25), calls=%async_computation.15 | async-start | bytes 524288 | tf_op jit(solution)/shard_map/all_to_all | solution.py:148
  354.2 8.7 %all-to-all-done.15 = f32[32,16,128]{2,1,0:T(8,128)} async-done(((f32[32,16,128]{2,1,0:T(8,128)}), f32[32,16,128]{2,1,0:T(8,128)}, u32[]{:S(2)}, u32[]{:S(2)}) %all-to-all-start.15) | async-done | bytes 262176 | tf_op jit(solution)/shard_map/all_to_all | solution.py:148
  369.5 6.2 %multiply_add_fusion.1 = f32[4,16,16,128]{3,2,1,0:T(8,128)} fusion(f32[4,16,16,128]{3,2,1,0:T(8,128)S(1)} %bitcast.180, f32[4,16,4,128]{3,2,1,0:T(4,128)} %get-tuple-element.80, f32[4,16,12,128]{3,2,1,0:T(8,128)} %get-tuple-element.82, f32[4,16,12,128]{3,2,1,0:T(8,128)} %get-tuple-element.81, f32[4,16,4,128]{3,2,1,0:T(4,128)} %get-tuple-element.79, ...), kind=kLoop, calls=%fused_computation.195 | loop fusion | flops 8126464 | bytes 10489856 | tf_op jit(solution)/shard_map/add | solution.py:216
  383.6 16.5 %all_to_all.141 = f32[32,1,384]{2,1,0:T(1,128)S(1)} all-to-all(f32[32,1,384]{2,1,0:T(1,128)S(1)} %broadcast_in_dim.88), channel_id=1, replica_groups=mesh['grid'=32,'band_0'=2,'band_1'=2] {'grid'}, dimensions={0} | all-to-all | bytes 98304 | tf_op jit(solution)/shard_map/all_to_all | solution.py:115
  407.8 9.8 %all-to-all-done.18 = f32[2,4,16,16,128]{4,3,2,1,0:T(8,128)} async-done(((f32[2,4,16,16,128]{4,3,2,1,0:T(8,128)}), f32[2,4,16,16,128]{4,3,2,1,0:T(8,128)}, u32[]{:S(2)}, u32[]{:S(2)}) %all-to-all-start.18) | async-done | bytes 1048608 | tf_op jit(solution)/shard_map/all_to_all | solution.py:115
  421.0 5.4 all_to_all.142
  435.7 14.3 %all_to_all.143 = f32[32,4,512]{2,1,0:T(4,128)S(1)} all-to-all(f32[32,4,512]{2,1,0:T(4,128)S(1)} %copy.239), channel_id=1, replica_groups=mesh['grid'=32,'band_0'=2,'band_1'=2] {'grid'}, dimensions={0} | all-to-all | bytes 524288 | tf_op jit(solution)/shard_map/all_to_all | solution.py:148
  450.1 14.2 %all_to_all.144 = f32[32,4,512]{2,1,0:T(4,128)S(1)} all-to-all(f32[32,4,512]{2,1,0:T(4,128)S(1)} %broadcast_in_dim.91), channel_id=1, replica_groups=mesh['grid'=32,'band_0'=2,'band_1'=2] {'grid'}, dimensions={0} | all-to-all | bytes 524288 | tf_op jit(solution)/shard_map/all_to_all | solution.py:115
  464.5 17.8 %all_to_all.145 = f32[4,128,512]{2,1,0:T(8,128)} all-to-all(f32[4,128,512]{2,1,0:T(8,128)S(1)} %broadcast_in_dim.92), channel_id=1, replica_groups=mesh['grid'=32,'band_0'=2,'band_1'=2] {'band_0','band_1'}, dimensions={0} | all-to-all | bytes 2097152 | tf_op jit(solution)/shard_map/all_to_all | solution.py:115
  482.3 22.4 %inverse_factor.5 = f32[512,512]{1,0:T(8,128)} custom-call(f32[512,512]{1,0:T(8,128)} %bitcast.225), custom_call_target="tpu_custom_call" | custom-call | flops 20000000000 | bytes 2097152 | tf_op jit(solution)/shard_map/inverse_factor/pallas_call | solution.py:89
  525.1 9.6 %all-to-all-start.23 = ((f32[32,16,128]{2,1,0:T(8,128)}), f32[32,16,128]{2,1,0:T(8,128)}, u32[]{:S(2)}, u32[]{:S(2)}) async-start(f32[32,16,128]{2,1,0:T(8,128)} %bitcast.37), calls=%async_computation.23 | async-start | bytes 524288 | tf_op jit(solution)/shard_map/all_to_all | solution.py:148
  536.6 8.7 %all-to-all-done.23 = f32[32,16,128]{2,1,0:T(8,128)} async-done(((f32[32,16,128]{2,1,0:T(8,128)}), f32[32,16,128]{2,1,0:T(8,128)}, u32[]{:S(2)}, u32[]{:S(2)}) %all-to-all-start.23) | async-done | bytes 262176 | tf_op jit(solution)/shard_map/all_to_all | solution.py:148
  551.8 6.2 %multiply_add_fusion = f32[4,16,16,128]{3,2,1,0:T(8,128)} fusion(f32[4,16,16,128]{3,2,1,0:T(8,128)S(1)} %bitcast.161, f32[4,16,4,128]{3,2,1,0:T(4,128)} %get-tuple-element.48, f32[4,16,12,128]{3,2,1,0:T(8,128)} %get-tuple-element.50, f32[4,16,12,128]{3,2,1,0:T(8,128)} %get-tuple-element.49, f32[4,16,4,128]{3,2,1,0:T(4,128)} %get-tuple-element.47, ...), kind=kLoop, calls=%fused_computation.190 | loop fusion | flops 8126464 | bytes 10489856 | tf_op jit(solution)/shard_map/add | solution.py:216
  566.0 16.5 %all_to_all.146 = f32[32,1,384]{2,1,0:T(1,128)S(1)} all-to-all(f32[32,1,384]{2,1,0:T(1,128)S(1)} %broadcast_in_dim.94), channel_id=1, replica_groups=mesh['grid'=32,'band_0'=2,'band_1'=2] {'grid'}, dimensions={0} | all-to-all | bytes 98304 | tf_op jit(solution)/shard_map/all_to_all | solution.py:115
  (178 shorter events, 184.3 us)
Async XLA Ops:
  0.6 5.8 copy-start.1
  2.8 17.3 %all-to-all-start = ((f32[2,4,16,16,128]{4,3,2,1,0:T(8,128)}), f32[2,4,16,16,128]{4,3,2,1,0:T(8,128)S(1)}, u32[]{:S(2)}, u32[]{:S(2)}) async-start(f32[2,4,16,16,128]{4,3,2,1,0:T(8,128)} %broadcast_in_dim.75), calls=%async_computation | async-start | bytes 2097152 | tf_op jit(solution)/shard_map/all_to_all | solution.py:115
  29.3 5.1 copy-start
  31.3 25.0 %copy-start.3 = (f32[4,16,16,128]{3,2,1,0:T(8,128)S(1)}, f32[4,16,16,128]{3,2,1,0:T(8,128)}, u32[]{:S(2)}) copy-start(f32[4,16,16,128]{3,2,1,0:T(8,128)} %param.4) | copy-start | bytes 1572868
  57.4 16.0 %all-to-all-start.5 = ((f32[2,4,16,16,128]{4,3,2,1,0:T(8,128)}), f32[2,4,16,16,128]{4,3,2,1,0:T(8,128)S(1)}, u32[]{:S(2)}, u32[]{:S(2)}) async-start(f32[2,4,16,16,128]{4,3,2,1,0:T(8,128)} %broadcast_in_dim.79), calls=%async_computation.5 | async-start | bytes 2097152 | tf_op jit(solution)/shard_map/all_to_all | solution.py:115
  89.7 6.6 %all-to-all-start.6 = ((f32[2,2,4,16,16,128]{5,4,3,2,1,0:T(8,128)}), f32[2,2,4,16,16,128]{5,4,3,2,1,0:T(8,128)S(1)}, u32[]{:S(2)}, u32[]{:S(2)}) async-start(f32[2,2,4,16,16,128]{5,4,3,2,1,0:T(8,128)} %broadcast_in_dim.80), calls=%async_computation.6 | async-start | bytes 4194304 | tf_op jit(solution)/shard_map/all_to_all | solution.py:115
  97.5 18.1 %all-to-all-start.4 = ((f32[4,128,512]{2,1,0:T(8,128)}), f32[4,128,512]{2,1,0:T(8,128)S(1)}, u32[]{:S(2)}, u32[]{:S(2)}) async-start(f32[4,128,512]{2,1,0:T(8,128)} %broadcast_in_dim.78), calls=%async_computation.4 | async-start | bytes 2097152 | tf_op jit(solution)/shard_map/all_to_all | solution.py:115
  115.6 1.0 copy-start.2
  154.3 31.8 %collective-permute-start = (f32[4,16,16,128]{3,2,1,0:T(8,128)S(1)}, f32[4,16,16,128]{3,2,1,0:T(8,128)}, u32[]{:S(2)}, u32[]{:S(2)}) collective-permute-start(f32[4,16,16,128]{3,2,1,0:T(8,128)S(1)} %bitcast.194), channel_id=1, source_target_pairs={{4,0},{8,4},{12,8},{16,12},{20,16},{24,20},{28,24},{32,28},{36,32}... | collective-permute-start | bytes 1572872 | tf_op jit(solution)/shard_map/ppermute | solution.py:108
  156.5 29.6 %collective-permute-start.1 = (f32[4,16,16,128]{3,2,1,0:T(8,128)S(1)}, f32[4,16,16,128]{3,2,1,0:T(8,128)}, u32[]{:S(2)}, u32[]{:S(2)}) collective-permute-start(f32[4,16,16,128]{3,2,1,0:T(8,128)S(1)} %bitcast.195), channel_id=1, source_target_pairs={{0,4},{4,8},{8,12},{12,16},{16,20},{20,24},{24,28},{28,32},{32,36}... | collective-permute-start | bytes 1572872 | tf_op jit(solution)/shard_map/ppermute | solution.py:105
  159.3 20.1 %all-to-all-start.7 = ((f32[32,16,128]{2,1,0:T(8,128)}), f32[32,16,128]{2,1,0:T(8,128)}, u32[]{:S(2)}, u32[]{:S(2)}) async-start(f32[32,16,128]{2,1,0:T(8,128)} %bitcast.13), calls=%async_computation.7 | async-start | bytes 524288 | tf_op jit(solution)/shard_map/all_to_all | solution.py:148
  181.1 15.5 %all-to-all-start.8 = ((f32[32,16,128]{2,1,0:T(8,128)}), f32[32,16,128]{2,1,0:T(8,128)}, u32[]{:S(2)}, u32[]{:S(2)}) async-start(f32[32,16,128]{2,1,0:T(8,128)} %broadcast_in_dim.81), calls=%async_computation.8 | async-start | bytes 524288 | tf_op jit(solution)/shard_map/all_to_all | solution.py:115
  219.4 15.8 %all-to-all-start.10 = ((f32[2,4,16,16,128]{4,3,2,1,0:T(8,128)}), f32[2,4,16,16,128]{4,3,2,1,0:T(8,128)}, u32[]{:S(2)}, u32[]{:S(2)}) async-start(f32[2,4,16,16,128]{4,3,2,1,0:T(8,128)} %broadcast_in_dim.83), calls=%async_computation.10 | async-start | bytes 2097152 | tf_op jit(solution)/shard_map/all_to_all | solution.py:115
  332.6 36.8 %collective-permute-start.2 = (f32[4,16,16,128]{3,2,1,0:T(8,128)S(1)}, f32[4,16,16,128]{3,2,1,0:T(8,128)}, u32[]{:S(2)}, u32[]{:S(2)}) collective-permute-start(f32[4,16,16,128]{3,2,1,0:T(8,128)S(1)} %bitcast.168), channel_id=1, source_target_pairs={{4,0},{8,4},{12,8},{16,12},{20,16},{24,20},{28,24},{32,28},{36,32}... | collective-permute-start | bytes 1572872 | tf_op jit(solution)/shard_map/ppermute | solution.py:108
  334.8 34.6 %collective-permute-start.3 = (f32[4,16,16,128]{3,2,1,0:T(8,128)S(1)}, f32[4,16,16,128]{3,2,1,0:T(8,128)}, u32[]{:S(2)}, u32[]{:S(2)}) collective-permute-start(f32[4,16,16,128]{3,2,1,0:T(8,128)S(1)} %bitcast.169), channel_id=1, source_target_pairs={{0,4},{4,8},{8,12},{12,16},{16,20},{20,24},{24,28},{28,32},{32,36}... | collective-permute-start | bytes 1572872 | tf_op jit(solution)/shard_map/ppermute | solution.py:105
  342.8 20.1 %all-to-all-start.15 = ((f32[32,16,128]{2,1,0:T(8,128)}), f32[32,16,128]{2,1,0:T(8,128)}, u32[]{:S(2)}, u32[]{:S(2)}) async-start(f32[32,16,128]{2,1,0:T(8,128)} %bitcast.25), calls=%async_computation.15 | async-start | bytes 524288 | tf_op jit(solution)/shard_map/all_to_all | solution.py:148
  364.6 15.3 %all-to-all-start.16 = ((f32[32,16,128]{2,1,0:T(8,128)}), f32[32,16,128]{2,1,0:T(8,128)}, u32[]{:S(2)}, u32[]{:S(2)}) async-start(f32[32,16,128]{2,1,0:T(8,128)} %broadcast_in_dim.87), calls=%async_computation.16 | async-start | bytes 524288 | tf_op jit(solution)/shard_map/all_to_all | solution.py:115
  376.9 6.7 %copy-start.7 = (f32[128]{0:T(128)S(1)}, f32[128]{0:T(128)}, u32[]{:S(2)}) copy-start(f32[128]{0:T(128)} %get-tuple-element.128) | copy-start | bytes 1540
  403.2 14.4 %all-to-all-start.18 = ((f32[2,4,16,16,128]{4,3,2,1,0:T(8,128)}), f32[2,4,16,16,128]{4,3,2,1,0:T(8,128)}, u32[]{:S(2)}, u32[]{:S(2)}) async-start(f32[2,4,16,16,128]{4,3,2,1,0:T(8,128)} %broadcast_in_dim.89), calls=%async_computation.18 | async-start | bytes 2097152 | tf_op jit(solution)/shard_map/all_to_all | solution.py:115
  514.9 36.9 %collective-permute-start.4 = (f32[4,16,16,128]{3,2,1,0:T(8,128)S(1)}, f32[4,16,16,128]{3,2,1,0:T(8,128)}, u32[]{:S(2)}, u32[]{:S(2)}) collective-permute-start(f32[4,16,16,128]{3,2,1,0:T(8,128)S(1)} %bitcast.149), channel_id=1, source_target_pairs={{4,0},{8,4},{12,8},{16,12},{20,16},{24,20},{28,24},{32,28},{36,32}... | collective-permute-start | bytes 1572872 | tf_op jit(solution)/shard_map/ppermute | solution.py:108
  517.1 34.7 %collective-permute-start.5 = (f32[4,16,16,128]{3,2,1,0:T(8,128)S(1)}, f32[4,16,16,128]{3,2,1,0:T(8,128)}, u32[]{:S(2)}, u32[]{:S(2)}) collective-permute-start(f32[4,16,16,128]{3,2,1,0:T(8,128)S(1)} %bitcast.150), channel_id=1, source_target_pairs={{0,4},{4,8},{8,12},{12,16},{16,20},{20,24},{24,28},{28,32},{32,36}... | collective-permute-start | bytes 1572872 | tf_op jit(solution)/shard_map/ppermute | solution.py:105
  525.1 20.1 %all-to-all-start.23 = ((f32[32,16,128]{2,1,0:T(8,128)}), f32[32,16,128]{2,1,0:T(8,128)}, u32[]{:S(2)}, u32[]{:S(2)}) async-start(f32[32,16,128]{2,1,0:T(8,128)} %bitcast.37), calls=%async_computation.23 | async-start | bytes 524288 | tf_op jit(solution)/shard_map/all_to_all | solution.py:148
  546.9 15.4 %all-to-all-start.24 = ((f32[32,16,128]{2,1,0:T(8,128)}), f32[32,16,128]{2,1,0:T(8,128)}, u32[]{:S(2)}, u32[]{:S(2)}) async-start(f32[32,16,128]{2,1,0:T(8,128)} %broadcast_in_dim.93), calls=%async_computation.24 | async-start | bytes 524288 | tf_op jit(solution)/shard_map/all_to_all | solution.py:115
  559.2 6.8 %copy-start.6 = (f32[128]{0:T(128)S(1)}, f32[128]{0:T(128)}, u32[]{:S(2)}) copy-start(f32[128]{0:T(128)} %get-tuple-element.131) | copy-start | bytes 1540
  566.0 18.9 %copy-start.4 = (f32[1,128]{1,0:T(1,128)S(1)}, f32[1,128]{1,0:T(1,128)}, u32[]{:S(2)}) copy-start(f32[1,128]{1,0:T(1,128)} %get-tuple-element.119) | copy-start | bytes 1540
  566.0 18.9 %copy-start.5 = (f32[1,128]{1,0:T(1,128)S(1)}, f32[1,128]{1,0:T(1,128)}, u32[]{:S(2)}) copy-start(f32[1,128]{1,0:T(1,128)} %get-tuple-element.121) | copy-start | bytes 1540

commit v2 on v1

v2 whole, which is shorter than its diff:
```python
import jax
import jax.numpy as jnp
from jax import lax
from jax.experimental import pallas as pl
from jax.experimental.pallas import tpu as pltpu
from jax.sharding import Mesh
from jax.sharding import PartitionSpec as P

ITERS = 3
BAND = ("band_0", "band_1")
EVERY = ("grid", "band_0", "band_1")
BLOCK = 128
TILE = 8

STENCIL = (-205.0 / 72.0, 8.0 / 5.0, -1.0 / 5.0, 8.0 / 315.0, -1.0 / 560.0)
STEP_LENGTH = 0.25
NORM_EPS = 1e-06
HIGHEST = lax.Precision.HIGHEST
WHOLE = pl.BlockSpec(memory_space=pltpu.VMEM)


def dot(left, right, sides):
    return lax.dot_general(
        left, right, ((sides[:1], sides[1:]), ((), ())), precision=HIGHEST,
        preferred_element_type=jnp.float32,
    )


def row_of(tile, j):
    return jnp.broadcast_to(tile[j:j + 1, :], tile.shape)

def lane_of(tile, j):
    return jnp.broadcast_to(tile[:, j:j + 1], tile.shape)

def inverse_factor(tiles):
    count = len(tiles)
    lane = lax.broadcasted_iota(jnp.int32, tiles[0].shape, 1)
    sub = lax.broadcasted_iota(jnp.int32, tiles[0].shape, 0)
    tiles = list(tiles)
    for p in range(count):
        base = TILE * p
        inside = (lane >= base) & (lane < base + TILE)
        head = [lane_of(tiles[p], base + j) for j in range(TILE)]
        own = jnp.where(inside, (lane == base + sub).astype(jnp.float32), tiles[p])
        rows, scales, crosses = [], [], []
        for j in range(TILE):
            scale = lax.rsqrt(row_of(head[j], j))
            row = row_of(own, j) * scale
            column = jnp.where(sub > j, head[j] * scale, 0.0)
            own = jnp.where(sub == j, row, own - column * row)
            cross = [None] * TILE
            for k in range(j + 1, TILE):
                cross[k] = row_of(head[k], j) * scale
                head[k] = head[k] - column * cross[k]
            rows.append(row)
            scales.append(scale)
            crosses.append(cross)
        tiles[p] = jnp.where(lane < base + TILE, own, 0.0)
        for t in range(p + 1, count):
            parts = [lane_of(tiles[t], base + j) for j in range(TILE)]
            tile = jnp.where(inside, 0.0, tiles[t])
            for j in range(TILE):
                column = parts[j] * scales[j]
                tile = tile - column * rows[j]
                for k in range(j + 1, TILE):
                    parts[k] = parts[k] - column * crosses[j][k]
            tiles[t] = tile
    return tiles


def pairs_of(blocks):
    return [(i, j) for i in range(blocks) for j in range(i, blocks)]


def factor_kernel(s_ref, x_ref):
    blocks = x_ref.shape[0] // BLOCK
    for at, (i, j) in enumerate(pairs_of(blocks)):
        x_ref[BLOCK * i : BLOCK * (i + 1), BLOCK * j : BLOCK * (j + 1)] = s_ref[
            BLOCK * at : BLOCK * (at + 1), :
        ]

    def step(k, carry):
        here = pl.ds(pl.multiple_of(k * BLOCK, BLOCK), BLOCK)
        tiles = [
            x_ref[pl.ds(pl.multiple_of(k * BLOCK + TILE * t, TILE), TILE), here]
            for t in range(BLOCK // TILE)
        ]
        own = jnp.concatenate(inverse_factor(tiles), axis=0)
        x_ref[here, here] = jnp.eye(BLOCK, dtype=jnp.float32)
        x_ref[here, :] = dot(own, x_ref[here, :], (1, 0))

        def update(i, carry):
            there = pl.ds(pl.multiple_of(i * BLOCK, BLOCK), BLOCK)
            x_ref[there, here] = jnp.zeros((BLOCK, BLOCK), jnp.float32)
            x_ref[there, :] = x_ref[there, :] - dot(x_ref[here, there], x_ref[here, :], (0, 0))
            return carry

        return lax.fori_loop(k + 1, blocks, update, carry)

    for i in range(1, blocks):
        x_ref[BLOCK * i : BLOCK * (i + 1), : BLOCK * i] = jnp.zeros((BLOCK, BLOCK * i), jnp.float32)
    lax.fori_loop(0, blocks, step, 0)
    for i in range(blocks - 1):
        x_ref[BLOCK * i : BLOCK * (i + 1), BLOCK * (i + 1) :] = jnp.zeros(
            (BLOCK, BLOCK * (blocks - 1 - i)), jnp.float32
        )


def inverse_cholesky(s, size):
    return pl.pallas_call(
        factor_kernel,
        out_shape=jax.ShapeDtypeStruct((size, size), jnp.float32),
        in_specs=[WHOLE],
        out_specs=WHOLE,
        name="inverse_factor",
        cost_estimate=pl.CostEstimate(
            flops=20_000_000_000, bytes_accessed=2 * size * size * 4, transcendentals=size
        ),
    )(s)


def joined(ref):
    return jnp.concatenate([ref[b] for b in range(ref.shape[0])], axis=1)


def write_gram(v, xi, s_ref, c_ref):
    blocks = v.shape[1] // BLOCK
    at = 0
    for i in range(blocks):
        row = dot(v[:, BLOCK * i : BLOCK * (i + 1)], v[:, BLOCK * i :], (0, 0))
        for j in range(blocks - i):
            s_ref[BLOCK * at : BLOCK * (at + 1), :] = row[:, BLOCK * j : BLOCK * (j + 1)]
            at += 1
    c = dot(xi, v, (0, 0))
    for j in range(blocks):
        c_ref[j] = c[:, BLOCK * j : BLOCK * (j + 1)]


def gram_kernel(v_ref, xi_ref, s_ref, c_ref):
    write_gram(joined(v_ref), joined(xi_ref), s_ref, c_ref)


def stepped(vp, w, totals, blocks):
    rayleigh, energy, weight = (
        jnp.concatenate([totals[blocks * k + b : blocks * k + b + 1] for b in range(blocks)], axis=1)
        for k in range(3)
    )
    squared = energy - 2.0 * rayleigh * rayleigh + rayleigh * rayleigh * weight
    squared = jnp.maximum(squared, 0.0)
    factor = STEP_LENGTH / jnp.sqrt(squared + NORM_EPS)
    return vp - (w - rayleigh * vp) * factor, squared


def step_kernel(vp_ref, w_ref, sums_ref, xi_ref, v_ref, totals_ref, s_ref, c_ref):
    blocks = vp_ref.shape[0]
    totals = jnp.sum(sums_ref[...], axis=0)
    v, squared = stepped(joined(vp_ref), joined(w_ref), totals, blocks)
    for b in range(blocks):
        v_ref[b] = v[:, BLOCK * b : BLOCK * (b + 1)]
    totals_ref[...] = totals
    write_gram(v, joined(xi_ref), s_ref, c_ref)


def last_kernel(vp_ref, w_ref, sums_ref, v_ref, totals_ref):
    blocks = vp_ref.shape[0]
    totals = jnp.sum(sums_ref[...], axis=0)
    v, squared = stepped(joined(vp_ref), joined(w_ref), totals, blocks)
    for b in range(blocks):
        v_ref[b] = v[:, BLOCK * b : BLOCK * (b + 1)]
    totals_ref[...] = totals


def transform_kernel(x_ref, c_ref, v_ref, u_ref, xi_ref, vp_ref, w_ref, sums_ref):
    blocks = v_ref.shape[0]
    x = x_ref[...]
    vp = dot(joined(v_ref), x, (1, 1))
    z = joined(u_ref) - dot(joined(xi_ref), joined(c_ref), (1, 0))
    w = dot(z, x, (1, 1))
    for b in range(blocks):
        vp_ref[b] = vp[:, BLOCK * b : BLOCK * (b + 1)]
        w_ref[b] = w[:, BLOCK * b : BLOCK * (b + 1)]
    for k, product in enumerate((vp * w, w * w, vp * vp)):
        total = jnp.sum(product, axis=0, keepdims=True)
        for b in range(blocks):
            sums_ref[blocks * k + b : blocks * k + b + 1, :] = total[:, BLOCK * b : BLOCK * (b + 1)]


def stencil_kernel(v_ref, below_ref, above_ref, left_ref, right_ref, p_ref, u_ref):
    planes, rows = v_ref.shape[1:3]
    along_z = [(below_ref, z) for z in range(planes)] + [(v_ref, z) for z in range(planes)]
    along_z += [(above_ref, z) for z in range(planes)]
    along_x = [(left_ref, x) for x in range(rows)] + [(v_ref, x) for x in range(rows)]
    along_x += [(right_ref, x) for x in range(rows)]
    for z in range(planes):
        for x in range(rows):
            centre = v_ref[0, z, x]
            count = centre.shape[0]
            total = 3.0 * STENCIL[0] * centre
            for d in range(1, 5):
                group = pltpu.roll(centre, d, 0) + pltpu.roll(centre, count - d, 0)
                for way in (d, -d):
                    ref, at = along_z[planes + z + way]
                    group = group + ref[0, at, x]
                    ref, at = along_x[rows + x + way]
                    group = group + ref[0, z, at]
                total = total + STENCIL[d] * group
            u_ref[0, z, x] = p_ref[z, x] * centre - 0.5 * total


def ring(count, by):
    return [(i, (i + by) % count) for i in range(count)]


def applied(v, potential):
    below = lax.ppermute(v, "grid", ring(lax.axis_size("grid"), 1))
    above = lax.ppermute(v, "grid", ring(lax.axis_size("grid"), -1))
    left = lax.ppermute(v, BAND, ring(lax.axis_size(BAND), 1))
    right = lax.ppermute(v, BAND, ring(lax.axis_size(BAND), -1))
    block = pl.BlockSpec((1, *v.shape[1:]), lambda b: (b, 0, 0, 0, 0))
    return pl.pallas_call(
        stencil_kernel,
        grid=(v.shape[0],),
        out_shape=jax.ShapeDtypeStruct(v.shape, jnp.float32),
        in_specs=[block] * 5 + [pl.BlockSpec(potential.shape, lambda b: (0, 0, 0, 0))],
        out_specs=block,
        name="stencil",
        cost_estimate=pl.CostEstimate(
            flops=30 * v.size, bytes_accessed=24 * v.size, transcendentals=0
        ),
    )(v, below, above, left, right, potential)


def total_everywhere(parts):
    rows, lanes = parts.shape
    count = lax.axis_size(EVERY)
    pieces = parts.reshape(count, rows // count, lanes)
    arrived = lax.all_to_all(pieces, EVERY, split_axis=0, concat_axis=0, tiled=True)
    return from_everyone(arrived.sum(axis=0)).reshape(rows, lanes)


def from_everyone(x):
    copies = jnp.broadcast_to(x, (lax.axis_size(EVERY), *x.shape))
    return lax.all_to_all(copies, EVERY, split_axis=0, concat_axis=0, tiled=True)


def to_cells(field):
    z, x, y, lanes = field.shape
    count = lax.axis_size(BAND)
    pieces = jnp.moveaxis(field.reshape(z, count, x // count, y, lanes), 1, 0)
    return lax.all_to_all(pieces, BAND, split_axis=0, concat_axis=0, tiled=True)


def to_bands(field):
    count, z, x, y, lanes = field.shape
    pieces = lax.all_to_all(field, BAND, split_axis=0, concat_axis=0, tiled=True)
    return jnp.moveaxis(pieces, 0, 1).reshape(z, count * x, y, lanes)


def call(kernel, shapes, *args):
    return pl.pallas_call(
        kernel,
        out_shape=[jax.ShapeDtypeStruct(s, jnp.float32) for s in shapes],
        in_specs=[WHOLE] * len(args),
        out_specs=[WHOLE] * len(shapes),
        name=kernel.__name__,
        cost_estimate=pl.CostEstimate(
            flops=2_000_000_000, bytes_accessed=4 * sum(a.size for a in args), transcendentals=0
        ),
    )(*args)


def local(orbitals, projectors, potential):
    v5 = to_cells(orbitals)
    xi = to_cells(projectors)
    blocks, planes, rows, columns, lanes = v5.shape
    cells = planes * rows * columns
    flat = (blocks, cells, lanes)
    total = blocks * lanes
    xi = xi.reshape(flat)
    band = lax.axis_index(BAND)
    own = lax.dynamic_slice_in_dim(potential, band * rows, rows, 1)
    own = jnp.broadcast_to(own[..., None], (planes, rows, columns, lanes))
    s_shape = (len(pairs_of(blocks)) * BLOCK, BLOCK)
    c_shape = (blocks, total, BLOCK)
    v = v5.reshape(flat)
    s, c = call(gram_kernel, [s_shape, c_shape], v, xi)
    quotient_list = []
    norm_list = []
    for iteration in range(ITERS):
        u = applied(v.reshape(v5.shape), own).reshape(flat)
        s = total_everywhere(s)
        c = total_everywhere(c.reshape(-1, BLOCK)).reshape(c_shape)
        x = inverse_cholesky(s, total)
        vp, w, sums = call(transform_kernel, [flat, flat, (3 * blocks, BLOCK)], x, c, v, u, xi)
        everyone = from_everyone(sums)
        if iteration < ITERS - 1:
            v, totals, s, c = call(
                step_kernel, [flat, sums.shape, s_shape, c_shape], vp, w, everyone, xi
            )
        else:
            v, totals = call(last_kernel, [flat, sums.shape], vp, w, everyone)
        mine = lax.dynamic_slice_in_dim(totals.reshape(3, blocks, lanes), band, 1, 1)[:, 0]
        rayleigh, energy, weight = mine
        squared = energy - 2.0 * rayleigh * rayleigh + rayleigh * rayleigh * weight
        quotient_list.append(rayleigh)
        norm_list.append(jnp.sqrt(jnp.maximum(squared, 0.0)))
    return (to_bands(v.reshape(v5.shape)), jnp.stack(quotient_list), jnp.stack(norm_list))


def solution(mesh):
    finer = Mesh(mesh.devices.reshape(mesh.shape["grid"], 2, 2), ("grid", "band_0", "band_1"))
    placed = (P("grid", None, None, BAND), P("grid", None, None, BAND), P("grid", None, None))
    return jax.shard_map(
        local,
        mesh=finer,
        in_specs=placed,
        out_specs=(P("grid", None, None, BAND), P(None, BAND), P(None, BAND)),
        check_vma=False,
    )
```

time: 594 us -> 571 us (0.961)
  waiting for transfers between devices: 97.7 us -> 188 us
  local copies, waits for them, and re-layouts: 88.3 us -> 26.9 us
  blocking collectives: 195 us -> 147 us
  Pallas kernels: 67.3 us -> 112 us
  matrix products: 36.1 us -> 0 us
  other arithmetic: 26.6 us -> 2.04 us
  starting transfers between devices: 73.4 us -> 85.8 us
    ppermute x6 -> x12, waiting for transfers between devices: 0.02 us -> 97.2 us  [the longest x3 42 us: applied(): right = lax.ppermute(v, BAND, ring(lax.axis_size(BAND), -1))]
    all_to_all x14 -> x6, blocking collectives: 195 us -> 147 us  [the longest x3 77.5 us: total_everywhere(): lax.all_to_all(pieces, EVERY, split_axis=0, concat_axis=0, tiled=True)]
    pallas_call x3 -> x13, Pallas kernels: 67.3 us -> 112 us  [the longest x3 66.9 us: inverse_cholesky(): pl.pallas_call(factor_kernel, out_shape=jax.ShapeDtypeStruct((size, size)...]
    slice x48 -> x0, local copies, waits for them, and re-layouts: 40.9 us -> none  [laplacian(): jnp.roll(grid_field, distance, dimension)]
    dot_general x12 -> x0, matrix products: 36.1 us -> none  [matmul(): jnp.dot(left, right, precision=HIGHEST, preferred_element_type=jnp.float32)]
    ppermute x6 -> x12, starting transfers between devices: 6.54 us -> 26.2 us  [the longest x3 23.6 us: applied(): above = lax.ppermute(v, 'grid', ring(lax.axis_size('grid'), -1))]
    add x3 -> x0, other arithmetic: 18.5 us -> none  [local(): -0.5 * laplacian(grid_field) + potential[..., None] * grid_field]
    another operation x3 -> x2, local copies, waits for them, and re-layouts: 8.12 us -> 0.02 us  [local(): rayleigh, energy, weight = mine]
  transfers between devices with their start and end apart: 18 -> 24, of which waited for: 12 -> 18; matrix products, arithmetic and copies ran while one was open for 9% -> 1% of each run, Pallas kernels for 0% -> 14%
where the time goes in v2:
time: 571 us; the launch traced here: 563 us
  waiting for transfers between devices  188 us (33%)
  blocking collectives  147 us (26%)
  Pallas kernels  112 us (20%)
  starting transfers between devices  85.8 us (15%)
  local copies, waits for them, and re-layouts  26.9 us (5%)
    all_to_all x3, blocking collectives, total_everywhere(): lax.all_to_all(pieces, EVERY, split_axis=0, concat_axis=0, tiled=True)  77.5 us
    pallas_call x3, Pallas kernels, inverse_cholesky(): pl.pallas_call(factor_kernel, out_shape=jax.ShapeDtypeStruct((size, size)...  66.9 us
    all_to_all x2, blocking collectives, from_everyone(): lax.all_to_all(copies, EVERY, split_axis=0, concat_axis=0, tiled=True)  57.7 us
    all_to_all x3, waiting for transfers between devices, total_everywhere(): lax.all_to_all(pieces, EVERY, split_axis=0, concat_axis=0, tiled=True)  56.9 us
    ppermute x3, waiting for transfers between devices, applied(): right = lax.ppermute(v, BAND, ring(lax.axis_size(BAND), -1))  42 us
    all_to_all x7, starting transfers between devices, from_everyone(): lax.all_to_all(copies, EVERY, split_axis=0, concat_axis=0, tiled=True)  38.2 us
    pallas_call x7, Pallas kernels, call(): pl.pallas_call(kernel, out_shape=[jax.ShapeDtypeStruct(s, jnp.float32) fo...  32.7 us
    ppermute x3, waiting for transfers between devices, applied(): above = lax.ppermute(v, 'grid', ring(lax.axis_size('grid'), -1))  29.1 us
  transfers between devices with their start and end apart: 24, of which 18 were waited for; matrix products, arithmetic and copies ran while one was open for 1% of the time, Pallas kernels for 14%

profile of v2, /device:TPU:0, one launch (start us, length us, event | category | flops | bytes accessed | tf_op | source)
XLA Modules:
  0.0 563.2 jit_solution(15714835602107166678)
XLA Ops:
  6.2 8.7 %all-to-all-done.v_ref = f32[4,4,4,16,128]{4,3,2,1,0:T(8,128)S(1)} async-done(((f32[4,4,4,16,128]{4,3,2,1,0:T(8,128)}), f32[4,4,4,16,128]{4,3,2,1,0:T(8,128)S(1)}, u32[]{:S(2)}, u32[]{:S(2)}) %all-to-all-start) | async-done | bytes 524320 | tf_op jit(solution)/shard_map/all_to_all | solution.py:250
  14.9 11.9 %all_to_all.90 = f32[4,4,4,16,128]{4,3,2,1,0:T(8,128)} all-to-all(f32[4,4,4,16,128]{4,3,2,1,0:T(8,128)S(1)} %bitcast.81), channel_id=1, replica_groups=mesh['grid'=32,'band_0'=2,'band_1'=2] {'band_0','band_1'}, dimensions={0} | all-to-all | bytes 1048576 | tf_op jit(solution)/shard_map/all_to_all | solution.py:250
  31.9 30.1 %all_to_all.91 = f32[128,10,128]{2,1,0:T(8,128)S(1)} all-to-all(f32[128,10,128]{2,1,0:T(8,128)S(1)} %reshape.260), channel_id=1, replica_groups=mesh['grid'=32,'band_0'=2,'band_1'=2] {'grid','band_0','band_1'}, dimensions={0} | all-to-all | bytes 1310720 | tf_op jit(solution)/shard_map/all_to_all | solution.py:237
  66.9 19.0 %all-to-all-done.4 = f32[128,16,128]{2,1,0:T(8,128)S(1)} async-done(((f32[128,16,128]{2,1,0:T(8,128)}), f32[128,16,128]{2,1,0:T(8,128)S(1)}, u32[]{:S(2)}, u32[]{:S(2)}) %all-to-all-start.4) | async-done | bytes 1048608 | tf_op jit(solution)/shard_map/all_to_all | solution.py:237
  92.5 7.8 %collective-permute-start.1 = (f32[4,4,4,16,128]{4,3,2,1,0:T(8,128)S(1)}, f32[4,4,4,16,128]{4,3,2,1,0:T(8,128)}, u32[]{:S(2)}, u32[]{:S(2)}) collective-permute-start(f32[4,4,4,16,128]{4,3,2,1,0:T(8,128)S(1)} %copy-done.2), channel_id=1, source_target_pairs={{0,124},{4,0},{8,4},{12,8},{16,12},{20,16},{24,20},{28,24},{32,28}... | collective-permute-start | bytes 1572872 | tf_op jit(solution)/shard_map/ppermute | solution.py:216
  100.3 14.2 %collective-permute-done.3.right_ref = f32[4,4,4,16,128]{4,3,2,1,0:T(8,128)S(1)} collective-permute-done((f32[4,4,4,16,128]{4,3,2,1,0:T(8,128)S(1)}, f32[4,4,4,16,128]{4,3,2,1,0:T(8,128)S(1)}, u32[]{:S(2)}, u32[]{:S(2)}) %collective-permute-start.3) | collective-permute-done | bytes 524320 | tf_op jit(solution)/shard_map/ppermute | solution.py:218
  115.0 9.6 %collective-permute-done.1.above_ref = f32[4,4,4,16,128]{4,3,2,1,0:T(8,128)} collective-permute-done((f32[4,4,4,16,128]{4,3,2,1,0:T(8,128)S(1)}, f32[4,4,4,16,128]{4,3,2,1,0:T(8,128)}, u32[]{:S(2)}, u32[]{:S(2)}) %collective-permute-start.1) | collective-permute-done | bytes 524320 | tf_op jit(solution)/shard_map/ppermute | solution.py:216
  124.6 8.8 %collective-permute-done.below_ref = f32[4,4,4,16,128]{4,3,2,1,0:T(8,128)} collective-permute-done((f32[4,4,4,16,128]{4,3,2,1,0:T(8,128)S(1)}, f32[4,4,4,16,128]{4,3,2,1,0:T(8,128)}, u32[]{:S(2)}, u32[]{:S(2)}) %collective-permute-start) | collective-permute-done | bytes 524320 | tf_op jit(solution)/shard_map/ppermute | solution.py:215
  139.5 4.8 all-to-all-start.5
  145.2 22.3 %inverse_factor.3.x_ref = f32[512,512]{1,0:T(8,128)} custom-call(f32[1280,128]{1,0:T(8,128)} %reshape.261.s_ref), custom_call_target="tpu_custom_call" | custom-call | flops 20000000000 | bytes 2097152 | tf_op jit(solution)/shard_map/inverse_factor/pallas_call | solution.py:110
  168.5 5.7 %transform_kernel.3 = (f32[4,256,128]{2,1,0:T(8,128)}, f32[4,256,128]{2,1,0:T(8,128)}, f32[12,128]{1,0:T(8,128)}) custom-call(f32[512,512]{1,0:T(8,128)} %inverse_factor.3.x_ref, f32[4,512,128]{2,1,0:T(8,128)} %bitcast.83, f32[4,256,128]{2,1,0:T(8,128)} %bitcast.79, f32[4,256,128]{2,1,0:T(8,128)} %bitcast.96, f32[4,256,128]{2,1,0:T(8,128)} %bitcast.101), custom_call_target="tpu_custom_call" | custom-call | flops 2000000000 | bytes 3670016 | tf_op jit(solution)/shard_map/transform_kernel/pallas_call | solution.py:260
  175.0 28.9 %all_to_all.92.sums_ref = f32[128,12,128]{2,1,0:T(8,128)} all-to-all(f32[128,12,128]{2,1,0:T(8,128)S(1)} %broadcast_in_dim.36), channel_id=1, replica_groups=mesh['grid'=32,'band_0'=2,'band_1'=2] {'grid','band_0','band_1'}, dimensions={0} | all-to-all | bytes 1572864 | tf_op jit(solution)/shard_map/all_to_all | solution.py:243
  209.6 23.7 %all_to_all.93 = f32[128,10,128]{2,1,0:T(8,128)S(1)} all-to-all(f32[128,10,128]{2,1,0:T(8,128)S(1)} %reshape.263), channel_id=1, replica_groups=mesh['grid'=32,'band_0'=2,'band_1'=2] {'grid','band_0','band_1'}, dimensions={0} | all-to-all | bytes 1310720 | tf_op jit(solution)/shard_map/all_to_all | solution.py:237
  238.2 19.0 %all-to-all-done.9 = f32[128,16,128]{2,1,0:T(8,128)S(1)} async-done(((f32[128,16,128]{2,1,0:T(8,128)}), f32[128,16,128]{2,1,0:T(8,128)S(1)}, u32[]{:S(2)}, u32[]{:S(2)}) %all-to-all-start.9) | async-done | bytes 1048608 | tf_op jit(solution)/shard_map/all_to_all | solution.py:237
  264.2 7.9 %collective-permute-start.5 = (f32[4,4,4,16,128]{4,3,2,1,0:T(8,128)S(1)}, f32[4,4,4,16,128]{4,3,2,1,0:T(8,128)S(1)}, u32[]{:S(2)}, u32[]{:S(2)}) collective-permute-start(f32[4,4,4,16,128]{4,3,2,1,0:T(8,128)S(1)} %bitcast.93), channel_id=1, source_target_pairs={{0,124},{4,0},{8,4},{12,8},{16,12},{20,16},{24,20},{28,24},{32,28}... | collective-permute-start | bytes 1572872 | tf_op jit(solution)/shard_map/ppermute | solution.py:216
  272.1 13.7 %collective-permute-done.7.right_ref = f32[4,4,4,16,128]{4,3,2,1,0:T(8,128)S(1)} collective-permute-done((f32[4,4,4,16,128]{4,3,2,1,0:T(8,128)S(1)}, f32[4,4,4,16,128]{4,3,2,1,0:T(8,128)S(1)}, u32[]{:S(2)}, u32[]{:S(2)}) %collective-permute-start.7) | collective-permute-done | bytes 524320 | tf_op jit(solution)/shard_map/ppermute | solution.py:218
  286.2 9.7 %collective-permute-done.5.above_ref = f32[4,4,4,16,128]{4,3,2,1,0:T(8,128)S(1)} collective-permute-done((f32[4,4,4,16,128]{4,3,2,1,0:T(8,128)S(1)}, f32[4,4,4,16,128]{4,3,2,1,0:T(8,128)S(1)}, u32[]{:S(2)}, u32[]{:S(2)}) %collective-permute-start.5) | collective-permute-done | bytes 524320 | tf_op jit(solution)/shard_map/ppermute | solution.py:216
  296.7 8.0 %collective-permute-done.4.below_ref = f32[4,4,4,16,128]{4,3,2,1,0:T(8,128)} collective-permute-done((f32[4,4,4,16,128]{4,3,2,1,0:T(8,128)S(1)}, f32[4,4,4,16,128]{4,3,2,1,0:T(8,128)}, u32[]{:S(2)}, u32[]{:S(2)}) %collective-permute-start.4) | collective-permute-done | bytes 524320 | tf_op jit(solution)/shard_map/ppermute | solution.py:215
  315.6 22.3 %inverse_factor.4.x_ref = f32[512,512]{1,0:T(8,128)} custom-call(f32[1280,128]{1,0:T(8,128)} %reshape.264.s_ref), custom_call_target="tpu_custom_call" | custom-call | flops 20000000000 | bytes 2097152 | tf_op jit(solution)/shard_map/inverse_factor/pallas_call | solution.py:110
  338.9 5.7 %transform_kernel.4 = (f32[4,256,128]{2,1,0:T(8,128)}, f32[4,256,128]{2,1,0:T(8,128)}, f32[12,128]{1,0:T(8,128)}) custom-call(f32[512,512]{1,0:T(8,128)} %inverse_factor.4.x_ref, f32[4,512,128]{2,1,0:T(8,128)} %bitcast.84, f32[4,256,128]{2,1,0:T(8,128)} %get-tuple-element.31.v_ref, f32[4,256,128]{2,1,0:T(8,128)} %bitcast.97, f32[4,256,128]{2,1,0:T(8,128)} %bitcast.103), custom_call_target="tpu_custom_call" | custom-call | flops 2000000000 | bytes 3670016 | tf_op jit(solution)/shard_map/transform_kernel/pallas_call | solution.py:260
  345.4 28.8 %all_to_all.94.sums_ref = f32[128,12,128]{2,1,0:T(8,128)} all-to-all(f32[128,12,128]{2,1,0:T(8,128)S(1)} %broadcast_in_dim.39), channel_id=1, replica_groups=mesh['grid'=32,'band_0'=2,'band_1'=2] {'grid','band_0','band_1'}, dimensions={0} | all-to-all | bytes 1572864 | tf_op jit(solution)/shard_map/all_to_all | solution.py:243
  379.9 23.7 %all_to_all.95 = f32[128,10,128]{2,1,0:T(8,128)S(1)} all-to-all(f32[128,10,128]{2,1,0:T(8,128)S(1)} %reshape.267), channel_id=1, replica_groups=mesh['grid'=32,'band_0'=2,'band_1'=2] {'grid','band_0','band_1'}, dimensions={0} | all-to-all | bytes 1310720 | tf_op jit(solution)/shard_map/all_to_all | solution.py:237
  408.5 19.0 %all-to-all-done.14 = f32[128,16,128]{2,1,0:T(8,128)S(1)} async-done(((f32[128,16,128]{2,1,0:T(8,128)}), f32[128,16,128]{2,1,0:T(8,128)S(1)}, u32[]{:S(2)}, u32[]{:S(2)}) %all-to-all-start.14) | async-done | bytes 1048608 | tf_op jit(solution)/shard_map/all_to_all | solution.py:237
  434.1 7.8 %collective-permute-start.9 = (f32[4,4,4,16,128]{4,3,2,1,0:T(8,128)S(1)}, f32[4,4,4,16,128]{4,3,2,1,0:T(8,128)S(1)}, u32[]{:S(2)}, u32[]{:S(2)}) collective-permute-start(f32[4,4,4,16,128]{4,3,2,1,0:T(8,128)S(1)} %bitcast.88), channel_id=1, source_target_pairs={{0,124},{4,0},{8,4},{12,8},{16,12},{20,16},{24,20},{28,24},{32,28}... | collective-permute-start | bytes 1572872 | tf_op jit(solution)/shard_map/ppermute | solution.py:216
  441.9 14.2 %collective-permute-done.11.right_ref = f32[4,4,4,16,128]{4,3,2,1,0:T(8,128)S(1)} collective-permute-done((f32[4,4,4,16,128]{4,3,2,1,0:T(8,128)S(1)}, f32[4,4,4,16,128]{4,3,2,1,0:T(8,128)S(1)}, u32[]{:S(2)}, u32[]{:S(2)}) %collective-permute-start.11) | collective-permute-done | bytes 524320 | tf_op jit(solution)/shard_map/ppermute | solution.py:218
  456.5 9.7 %collective-permute-done.9.above_ref = f32[4,4,4,16,128]{4,3,2,1,0:T(8,128)S(1)} collective-permute-done((f32[4,4,4,16,128]{4,3,2,1,0:T(8,128)S(1)}, f32[4,4,4,16,128]{4,3,2,1,0:T(8,128)S(1)}, u32[]{:S(2)}, u32[]{:S(2)}) %collective-permute-start.9) | collective-permute-done | bytes 524320 | tf_op jit(solution)/shard_map/ppermute | solution.py:216
  467.0 8.0 %collective-permute-done.8.below_ref = f32[4,4,4,16,128]{4,3,2,1,0:T(8,128)} collective-permute-done((f32[4,4,4,16,128]{4,3,2,1,0:T(8,128)S(1)}, f32[4,4,4,16,128]{4,3,2,1,0:T(8,128)}, u32[]{:S(2)}, u32[]{:S(2)}) %collective-permute-start.8) | collective-permute-done | bytes 524320 | tf_op jit(solution)/shard_map/ppermute | solution.py:215
  486.0 22.3 %inverse_factor.5.x_ref = f32[512,512]{1,0:T(8,128)} custom-call(f32[1280,128]{1,0:T(8,128)} %reshape.268.s_ref), custom_call_target="tpu_custom_call" | custom-call | flops 20000000000 | bytes 2097152 | tf_op jit(solution)/shard_map/inverse_factor/pallas_call | solution.py:110
  509.3 5.7 %transform_kernel.5 = (f32[4,256,128]{2,1,0:T(8,128)}, f32[4,256,128]{2,1,0:T(8,128)}, f32[12,128]{1,0:T(8,128)}) custom-call(f32[512,512]{1,0:T(8,128)} %inverse_factor.5.x_ref, f32[4,512,128]{2,1,0:T(8,128)} %bitcast.82, f32[4,256,128]{2,1,0:T(8,128)} %get-tuple-element.37.v_ref, f32[4,256,128]{2,1,0:T(8,128)} %bitcast.95, f32[4,256,128]{2,1,0:T(8,128)} %bitcast.105), custom_call_target="tpu_custom_call" | custom-call | flops 2000000000 | bytes 3670016 | tf_op jit(solution)/shard_map/transform_kernel/pallas_call | solution.py:260
  516.7 9.8 %all-to-all-start.16 = ((f32[128,12,128]{2,1,0:T(8,128)}), f32[128,12,128]{2,1,0:T(8,128)S(1)}, u32[]{:S(2)}, u32[]{:S(2)}) async-start(f32[128,12,128]{2,1,0:T(8,128)} %broadcast_in_dim.42), calls=%async_computation.16 | async-start | bytes 2097152 | tf_op jit(solution)/shard_map/all_to_all | solution.py:243
  527.9 17.7 %all-to-all-done.16.sums_ref = f32[128,12,128]{2,1,0:T(8,128)S(1)} async-done(((f32[128,12,128]{2,1,0:T(8,128)}), f32[128,12,128]{2,1,0:T(8,128)S(1)}, u32[]{:S(2)}, u32[]{:S(2)}) %all-to-all-start.16) | async-done | bytes 786464 | tf_op jit(solution)/shard_map/all_to_all | solution.py:243
  554.6 7.6 %all-to-all-done.17 = f32[4,4,4,16,128]{4,3,2,1,0:T(8,128)S(1)} async-done(((f32[4,4,4,16,128]{4,3,2,1,0:T(8,128)}), f32[4,4,4,16,128]{4,3,2,1,0:T(8,128)S(1)}, u32[]{:S(2)}, u32[]{:S(2)}) %all-to-all-start.17) | async-done | bytes 524320 | tf_op jit(solution)/shard_map/all_to_all | solution.py:255
  (108 shorter events, 106.0 us)
Async XLA Ops:
  0.6 99.7 %copy-start = (f32[4,16,16]{2,1,0:T(8,128)S(1)}, f32[4,16,16]{2,1,0:T(8,128)}, u32[]{:S(2)}) copy-start(f32[4,16,16]{2,1,0:T(8,128)} %param.5) | copy-start | bytes 12292
  2.5 12.4 %all-to-all-start = ((f32[4,4,4,16,128]{4,3,2,1,0:T(8,128)}), f32[4,4,4,16,128]{4,3,2,1,0:T(8,128)S(1)}, u32[]{:S(2)}, u32[]{:S(2)}) async-start(f32[4,4,4,16,128]{4,3,2,1,0:T(8,128)} %bitcast.77), calls=%async_computation | async-start | bytes 1048576 | tf_op jit(solution)/shard_map/all_to_all | solution.py:250
  14.9 11.9 %copy-start.1 = (f32[4,4,4,16,128]{4,3,2,1,0:T(8,128)}, f32[4,4,4,16,128]{4,3,2,1,0:T(8,128)S(1)}, u32[]{:S(2)}) copy-start(f32[4,4,4,16,128]{4,3,2,1,0:T(8,128)S(1)} %all-to-all-done.v_ref) | copy-start | bytes 1572868
  62.0 23.9 %all-to-all-start.4 = ((f32[128,16,128]{2,1,0:T(8,128)}), f32[128,16,128]{2,1,0:T(8,128)S(1)}, u32[]{:S(2)}, u32[]{:S(2)}) async-start(f32[128,16,128]{2,1,0:T(8,128)} %bitcast.6), calls=%async_computation.4 | async-start | bytes 2097152 | tf_op jit(solution)/shard_map/all_to_all | solution.py:237
  86.9 4.8 copy-start.2
  86.9 51.6 %all-to-all-start.3 = ((f32[128,10,128]{2,1,0:T(8,128)}), f32[128,10,128]{2,1,0:T(8,128)S(1)}, u32[]{:S(2)}, u32[]{:S(2)}) async-start(f32[128,10,128]{2,1,0:T(8,128)} %broadcast_in_dim.33), calls=%async_computation.3 | async-start | bytes 2097152 | tf_op jit(solution)/shard_map/all_to_all | solution.py:243
  91.7 22.7 %collective-permute-start.3 = (f32[4,4,4,16,128]{4,3,2,1,0:T(8,128)S(1)}, f32[4,4,4,16,128]{4,3,2,1,0:T(8,128)S(1)}, u32[]{:S(2)}, u32[]{:S(2)}) collective-permute-start(f32[4,4,4,16,128]{4,3,2,1,0:T(8,128)S(1)} %copy-done.2), channel_id=1, source_target_pairs={{0,3},{1,0},{2,1},{3,2},{4,7},{5,4},{6,5},{7,6},{8,11},{9,8},{10,9... | collective-permute-start | bytes 1572872 | tf_op jit(solution)/shard_map/ppermute | solution.py:218
  92.5 22.5 %collective-permute-start.2 = (f32[4,4,4,16,128]{4,3,2,1,0:T(8,128)S(1)}, f32[4,4,4,16,128]{4,3,2,1,0:T(8,128)}, u32[]{:S(2)}, u32[]{:S(2)}) collective-permute-start(f32[4,4,4,16,128]{4,3,2,1,0:T(8,128)S(1)} %copy-done.2), channel_id=1, source_target_pairs={{0,1},{1,2},{2,3},{3,0},{4,5},{5,6},{6,7},{7,4},{8,9},{9,10},{10,1... | collective-permute-start | bytes 1572872 | tf_op jit(solution)/shard_map/ppermute | solution.py:217
  92.5 32.1 %collective-permute-start.1 = (f32[4,4,4,16,128]{4,3,2,1,0:T(8,128)S(1)}, f32[4,4,4,16,128]{4,3,2,1,0:T(8,128)}, u32[]{:S(2)}, u32[]{:S(2)}) collective-permute-start(f32[4,4,4,16,128]{4,3,2,1,0:T(8,128)S(1)} %copy-done.2), channel_id=1, source_target_pairs={{0,124},{4,0},{8,4},{12,8},{16,12},{20,16},{24,20},{28,24},{32,28}... | collective-permute-start | bytes 1572872 | tf_op jit(solution)/shard_map/ppermute | solution.py:216
  100.3 33.1 %collective-permute-start = (f32[4,4,4,16,128]{4,3,2,1,0:T(8,128)S(1)}, f32[4,4,4,16,128]{4,3,2,1,0:T(8,128)}, u32[]{:S(2)}, u32[]{:S(2)}) collective-permute-start(f32[4,4,4,16,128]{4,3,2,1,0:T(8,128)S(1)} %copy-done.2), channel_id=1, source_target_pairs={{0,4},{4,8},{8,12},{12,16},{16,20},{20,24},{24,28},{28,32},{32,36}... | collective-permute-start | bytes 1572872 | tf_op jit(solution)/shard_map/ppermute | solution.py:215
  114.5 19.7 %copy-start.9 = (f32[4,4,4,16,128]{4,3,2,1,0:T(8,128)}, f32[4,4,4,16,128]{4,3,2,1,0:T(8,128)S(1)}, u32[]{:S(2)}) copy-start(f32[4,4,4,16,128]{4,3,2,1,0:T(8,128)S(1)} %collective-permute-done.3.right_ref) | copy-start | bytes 1572868
  139.5 28.0 %all-to-all-start.5 = ((f32[128,16,128]{2,1,0:T(8,128)}), f32[128,16,128]{2,1,0:T(8,128)S(1)}, u32[]{:S(2)}, u32[]{:S(2)}) async-start(f32[128,16,128]{2,1,0:T(8,128)} %broadcast_in_dim.34), calls=%async_computation.5 | async-start | bytes 2097152 | tf_op jit(solution)/shard_map/all_to_all | solution.py:243
  233.3 23.9 %all-to-all-start.9 = ((f32[128,16,128]{2,1,0:T(8,128)}), f32[128,16,128]{2,1,0:T(8,128)S(1)}, u32[]{:S(2)}, u32[]{:S(2)}) async-start(f32[128,16,128]{2,1,0:T(8,128)} %bitcast.9), calls=%async_computation.9 | async-start | bytes 2097152 | tf_op jit(solution)/shard_map/all_to_all | solution.py:237
  258.3 50.8 %all-to-all-start.8 = ((f32[128,10,128]{2,1,0:T(8,128)}), f32[128,10,128]{2,1,0:T(8,128)S(1)}, u32[]{:S(2)}, u32[]{:S(2)}) async-start(f32[128,10,128]{2,1,0:T(8,128)} %broadcast_in_dim.37), calls=%async_computation.8 | async-start | bytes 2097152 | tf_op jit(solution)/shard_map/all_to_all | solution.py:243
  263.1 22.7 %collective-permute-start.7 = (f32[4,4,4,16,128]{4,3,2,1,0:T(8,128)S(1)}, f32[4,4,4,16,128]{4,3,2,1,0:T(8,128)S(1)}, u32[]{:S(2)}, u32[]{:S(2)}) collective-permute-start(f32[4,4,4,16,128]{4,3,2,1,0:T(8,128)S(1)} %bitcast.91), channel_id=1, source_target_pairs={{0,3},{1,0},{2,1},{3,2},{4,7},{5,4},{6,5},{7,6},{8,11},{9,8},{10,9... | collective-permute-start | bytes 1572872 | tf_op jit(solution)/shard_map/ppermute | solution.py:218
  263.8 22.4 %collective-permute-start.6 = (f32[4,4,4,16,128]{4,3,2,1,0:T(8,128)S(1)}, f32[4,4,4,16,128]{4,3,2,1,0:T(8,128)S(1)}, u32[]{:S(2)}, u32[]{:S(2)}) collective-permute-start(f32[4,4,4,16,128]{4,3,2,1,0:T(8,128)S(1)} %bitcast.92), channel_id=1, source_target_pairs={{0,1},{1,2},{2,3},{3,0},{4,5},{5,6},{6,7},{7,4},{8,9},{9,10},{10,1... | collective-permute-start | bytes 1572872 | tf_op jit(solution)/shard_map/ppermute | solution.py:217
  264.2 31.7 %collective-permute-start.5 = (f32[4,4,4,16,128]{4,3,2,1,0:T(8,128)S(1)}, f32[4,4,4,16,128]{4,3,2,1,0:T(8,128)S(1)}, u32[]{:S(2)}, u32[]{:S(2)}) collective-permute-start(f32[4,4,4,16,128]{4,3,2,1,0:T(8,128)S(1)} %bitcast.93), channel_id=1, source_target_pairs={{0,124},{4,0},{8,4},{12,8},{16,12},{20,16},{24,20},{28,24},{32,28}... | collective-permute-start | bytes 1572872 | tf_op jit(solution)/shard_map/ppermute | solution.py:216
  272.1 32.6 %collective-permute-start.4 = (f32[4,4,4,16,128]{4,3,2,1,0:T(8,128)S(1)}, f32[4,4,4,16,128]{4,3,2,1,0:T(8,128)}, u32[]{:S(2)}, u32[]{:S(2)}) collective-permute-start(f32[4,4,4,16,128]{4,3,2,1,0:T(8,128)S(1)} %bitcast.94), channel_id=1, source_target_pairs={{0,4},{4,8},{8,12},{12,16},{16,20},{20,24},{24,28},{28,32},{32,36}... | collective-permute-start | bytes 1572872 | tf_op jit(solution)/shard_map/ppermute | solution.py:215
  285.8 18.9 %copy-start.11 = (f32[4,4,4,16,128]{4,3,2,1,0:T(8,128)}, f32[4,4,4,16,128]{4,3,2,1,0:T(8,128)S(1)}, u32[]{:S(2)}) copy-start(f32[4,4,4,16,128]{4,3,2,1,0:T(8,128)S(1)} %collective-permute-done.7.right_ref) | copy-start | bytes 1572868
  286.2 9.7 %copy-start.13 = (f32[4,4,4,16,128]{4,3,2,1,0:T(8,128)}, f32[4,4,4,16,128]{4,3,2,1,0:T(8,128)S(1)}, u32[]{:S(2)}) copy-start(f32[4,4,4,16,128]{4,3,2,1,0:T(8,128)S(1)} %collective-permute-done.6.left_ref) | copy-start | bytes 1572868
  310.1 27.8 %all-to-all-start.10 = ((f32[128,16,128]{2,1,0:T(8,128)}), f32[128,16,128]{2,1,0:T(8,128)S(1)}, u32[]{:S(2)}, u32[]{:S(2)}) async-start(f32[128,16,128]{2,1,0:T(8,128)} %broadcast_in_dim.38), calls=%async_computation.10 | async-start | bytes 2097152 | tf_op jit(solution)/shard_map/all_to_all | solution.py:243
  403.6 23.9 %all-to-all-start.14 = ((f32[128,16,128]{2,1,0:T(8,128)}), f32[128,16,128]{2,1,0:T(8,128)S(1)}, u32[]{:S(2)}, u32[]{:S(2)}) async-start(f32[128,16,128]{2,1,0:T(8,128)} %bitcast.13), calls=%async_computation.14 | async-start | bytes 2097152 | tf_op jit(solution)/shard_map/all_to_all | solution.py:237
  428.6 50.8 %all-to-all-start.13 = ((f32[128,10,128]{2,1,0:T(8,128)}), f32[128,10,128]{2,1,0:T(8,128)S(1)}, u32[]{:S(2)}, u32[]{:S(2)}) async-start(f32[128,10,128]{2,1,0:T(8,128)} %broadcast_in_dim.40), calls=%async_computation.13 | async-start | bytes 2097152 | tf_op jit(solution)/shard_map/all_to_all | solution.py:243
  433.4 22.7 %collective-permute-start.11 = (f32[4,4,4,16,128]{4,3,2,1,0:T(8,128)S(1)}, f32[4,4,4,16,128]{4,3,2,1,0:T(8,128)S(1)}, u32[]{:S(2)}, u32[]{:S(2)}) collective-permute-start(f32[4,4,4,16,128]{4,3,2,1,0:T(8,128)S(1)} %bitcast.86), channel_id=1, source_target_pairs={{0,3},{1,0},{2,1},{3,2},{4,7},{5,4},{6,5},{7,6},{8,11},{9,8},{10,9... | collective-permute-start | bytes 1572872 | tf_op jit(solution)/shard_map/ppermute | solution.py:218
  434.1 22.4 %collective-permute-start.10 = (f32[4,4,4,16,128]{4,3,2,1,0:T(8,128)S(1)}, f32[4,4,4,16,128]{4,3,2,1,0:T(8,128)S(1)}, u32[]{:S(2)}, u32[]{:S(2)}) collective-permute-start(f32[4,4,4,16,128]{4,3,2,1,0:T(8,128)S(1)} %bitcast.87), channel_id=1, source_target_pairs={{0,1},{1,2},{2,3},{3,0},{4,5},{5,6},{6,7},{7,4},{8,9},{9,10},{10,1... | collective-permute-start | bytes 1572872 | tf_op jit(solution)/shard_map/ppermute | solution.py:217
  434.1 32.1 %collective-permute-start.9 = (f32[4,4,4,16,128]{4,3,2,1,0:T(8,128)S(1)}, f32[4,4,4,16,128]{4,3,2,1,0:T(8,128)S(1)}, u32[]{:S(2)}, u32[]{:S(2)}) collective-permute-start(f32[4,4,4,16,128]{4,3,2,1,0:T(8,128)S(1)} %bitcast.88), channel_id=1, source_target_pairs={{0,124},{4,0},{8,4},{12,8},{16,12},{20,16},{24,20},{28,24},{32,28}... | collective-permute-start | bytes 1572872 | tf_op jit(solution)/shard_map/ppermute | solution.py:216
  441.9 33.1 %collective-permute-start.8 = (f32[4,4,4,16,128]{4,3,2,1,0:T(8,128)S(1)}, f32[4,4,4,16,128]{4,3,2,1,0:T(8,128)}, u32[]{:S(2)}, u32[]{:S(2)}) collective-permute-start(f32[4,4,4,16,128]{4,3,2,1,0:T(8,128)S(1)} %bitcast.89), channel_id=1, source_target_pairs={{0,4},{4,8},{8,12},{12,16},{16,20},{20,24},{24,28},{28,32},{32,36}... | collective-permute-start | bytes 1572872 | tf_op jit(solution)/shard_map/ppermute | solution.py:215
  456.1 18.9 %copy-start.10 = (f32[4,4,4,16,128]{4,3,2,1,0:T(8,128)}, f32[4,4,4,16,128]{4,3,2,1,0:T(8,128)S(1)}, u32[]{:S(2)}) copy-start(f32[4,4,4,16,128]{4,3,2,1,0:T(8,128)S(1)} %collective-permute-done.11.right_ref) | copy-start | bytes 1572868
  456.5 9.7 %copy-start.12 = (f32[4,4,4,16,128]{4,3,2,1,0:T(8,128)}, f32[4,4,4,16,128]{4,3,2,1,0:T(8,128)S(1)}, u32[]{:S(2)}) copy-start(f32[4,4,4,16,128]{4,3,2,1,0:T(8,128)S(1)} %collective-permute-done.10.left_ref) | copy-start | bytes 1572868
  480.4 27.9 %all-to-all-start.15 = ((f32[128,16,128]{2,1,0:T(8,128)}), f32[128,16,128]{2,1,0:T(8,128)S(1)}, u32[]{:S(2)}, u32[]{:S(2)}) async-start(f32[128,16,128]{2,1,0:T(8,128)} %broadcast_in_dim.41), calls=%async_computation.15 | async-start | bytes 2097152 | tf_op jit(solution)/shard_map/all_to_all | solution.py:243
  516.7 28.9 %all-to-all-start.16 = ((f32[128,12,128]{2,1,0:T(8,128)}), f32[128,12,128]{2,1,0:T(8,128)S(1)}, u32[]{:S(2)}, u32[]{:S(2)}) async-start(f32[128,12,128]{2,1,0:T(8,128)} %broadcast_in_dim.42), calls=%async_computation.16 | async-start | bytes 2097152 | tf_op jit(solution)/shard_map/all_to_all | solution.py:243
  549.9 12.3 %all-to-all-start.17 = ((f32[4,4,4,16,128]{4,3,2,1,0:T(8,128)}), f32[4,4,4,16,128]{4,3,2,1,0:T(8,128)S(1)}, u32[]{:S(2)}, u32[]{:S(2)}) async-start(f32[4,4,4,16,128]{4,3,2,1,0:T(8,128)} %bitcast.106), calls=%async_computation.17 | async-start | bytes 1048576 | tf_op jit(solution)/shard_map/all_to_all | solution.py:255
  (11 other events, 20.1 us)
